TPU v7x, 32 devices: a whole 2x2x4 slice. The times are simulated.
32 devices in a mesh: wide: 8 (over y, x, core), narrow: 4 (over z).
Axes of the slice: x: 2, y: 2, z: 4, core: 2. Of those that a mesh axis runs over, the one named last changes fastest.
Arguments:
- tokens: bfloat16 [8192, 2048], P(('wide', 'narrow')), may hold values from -6 to 6
- out_grad: bfloat16 [8192, 2048], P(('wide', 'narrow')), may hold values from -6 to 6
- captions: bfloat16 [4096, 4096], P(('wide', 'narrow')), may hold values from -6 to 6
- image_blocks: int32 [32, 256], P('wide'), may hold values from 0 to 3, never falling along the last dimension, each value on 1 to 128 neighbouring positions
- caption_owner: int32 [8, 512], P('wide'), may hold values from 0 to 3, never falling along the last dimension, each value on 1 to 256 neighbouring positions
- norm_gains: float32 [3, 2048], replicated, may hold values from 0.25 to 1.75
- norm_shifts: float32 [3, 2048], replicated, may hold values from -3 to 3
- w_query: float32 [2048, 2048], P('wide', 'narrow'), may hold values from -0.125 to 0.125
- w_key: float32 [2048, 2048], P('wide', 'narrow'), may hold values from -0.125 to 0.125
- w_value: float32 [2048, 2048], P('wide', 'narrow'), may hold values from -0.125 to 0.125
- w_out: float32 [2048, 2048], P('narrow', 'wide'), may hold values from -0.375 to 0.375
- w_cross_query: float32 [2048, 2048], P('wide', 'narrow'), may hold values from -0.125 to 0.125
- w_cross_key: float32 [4096, 2048], P('wide', 'narrow'), may hold values from -0.09375 to 0.09375
- w_cross_value: float32 [4096, 2048], P('wide', 'narrow'), may hold values from -0.09375 to 0.09375
- w_cross_out: float32 [2048, 2048], P('narrow', 'wide'), may hold values from -0.375 to 0.375
- w_up: float32 [2048, 8192], P('wide', 'narrow'), may hold values from -0.125 to 0.125
- w_down: float32 [8192, 2048], P('narrow', 'wide'), may hold values from -0.0625 to 0.0625
Outputs:
- block_out: bfloat16 [8192, 2048], P(('wide', 'narrow'))
- grad_tokens: bfloat16 [8192, 2048], P(('wide', 'narrow'))
- grad_captions: bfloat16 [4096, 4096], P(('wide', 'narrow'))
- grad_norm_gains: float32 [3, 2048], replicated
- grad_norm_shifts: float32 [3, 2048], replicated
- grad_w_query: float32 [2048, 2048], P('wide', 'narrow')
- grad_w_key: float32 [2048, 2048], P('wide', 'narrow')
- grad_w_value: float32 [2048, 2048], P('wide', 'narrow')
- grad_w_out: float32 [2048, 2048], P('narrow', 'wide')
- grad_w_cross_query: float32 [2048, 2048], P('wide', 'narrow')
- grad_w_cross_key: float32 [4096, 2048], P('wide', 'narrow')
- grad_w_cross_value: float32 [4096, 2048], P('wide', 'narrow')
- grad_w_cross_out: float32 [2048, 2048], P('narrow', 'wide')
- grad_w_up: float32 [2048, 8192], P('wide', 'narrow')
- grad_w_down: float32 [8192, 2048], P('narrow', 'wide')
Inputs may be any that keep to these rules, and one draw needn't show every extreme that they name: `image_blocks`: within an image the block numbers never fall; each of the 4 blocks has 1 to 128 tokens, and one block of every image has exactly that many. `caption_owner`: within a group the owners never fall; every image of the group has 1 to 256 caption tokens, and one image of every group has exactly 256.
All inputs are finite; a program needn't handle non-finite values.
Results may differ from a plain program's by a relative error of at most 0.024.
Values may be sent and summed in bfloat16 or wider, within the bound.
A program may use at most 320 MiB of HBM per device.

v0:
```python
import jax
import jax.numpy as jnp
from jax import lax
from jax.sharding import PartitionSpec as P

HEAD_DIM = 128
PIX = 256
CHUNKS = 2
EPSILON = 1e-06
MASKED = -1000000000.0
BF = jnp.bfloat16
F32 = jnp.float32


def product(left_side, right_side):
    return lax.dot_general(
        left_side, right_side, (((left_side.ndim - 1,), (0,)), ((), ())), preferred_element_type=F32
    )


def right_inner(left_side, right_side):
    return lax.dot_general(
        left_side, right_side, (((left_side.ndim - 1,), (1,)), ((), ())), preferred_element_type=F32
    )


def left_inner(left_side, right_side):
    rows = tuple(range(left_side.ndim - 1))
    return lax.dot_general(
        left_side, right_side, ((rows, rows), ((), ())), preferred_element_type=F32
    )


def spread(rows):
    n = lax.axis_size("narrow")
    here = lax.axis_index("narrow")
    up, down = ([rows], [rows])
    for step in range(1, n):
        up.append(lax.ppermute(up[-1], "narrow", [(k, k + 1) for k in range(step - 1, n - 1)]))
        down.append(lax.ppermute(down[-1], "narrow", [(k, k - 1) for k in range(1, n - step + 1)]))
    parts = [rows] + [jnp.where(here >= s, up[s], down[n - s]) for s in range(1, n)]
    return jnp.stack(parts)


def sink(parts):
    n = lax.axis_size("narrow")
    up = down = None
    for step in range(1, n):
        one, other = (parts[step], parts[n - step])
        if up is not None:
            one = up.astype(F32) + one.astype(F32)
            other = down.astype(F32) + other.astype(F32)
        up = lax.ppermute(one.astype(BF), "narrow", [(k, k + 1) for k in range(step)])
        down = lax.ppermute(other.astype(BF), "narrow", [(k, k - 1) for k in range(n - step, n)])
    return up.astype(F32) + down.astype(F32) + parts[0].astype(F32)


def norm_stats(features):
    center = features - jnp.mean(features, axis=-1, keepdims=True)
    rstd = lax.rsqrt(jnp.mean(center * center, axis=-1, keepdims=True) + EPSILON)
    return (center * rstd, rstd)


def norm_back(grad, xhat, rstd, gain):
    scaled = grad * gain
    return rstd * (
        scaled
        - jnp.mean(scaled, axis=-1, keepdims=True)
        - xhat * jnp.mean(scaled * xhat, axis=-1, keepdims=True)
    )


def norm_sums(grad, xhat):
    return jnp.stack([jnp.sum(grad * xhat, axis=0), jnp.sum(grad, axis=0)])


def score_block(queries, keys_in, allowed, score_scale):
    raw = jnp.einsum("iphe,iqhe->ihpq", queries, keys_in, preferred_element_type=F32)
    return jnp.where(allowed[:, None], raw * score_scale, MASKED)


def attend(queries, keys_in, values_in, allowed, score_scale):
    scores = score_block(queries, keys_in, allowed, score_scale)
    log_total = jax.nn.logsumexp(scores, axis=-1, keepdims=True)
    soft = jnp.exp(scores - log_total).astype(BF)
    mixture = jnp.einsum("ihpq,iqhe->iphe", soft, values_in, preferred_element_type=F32)
    return (mixture.astype(BF), log_total)


def attend_back(queries, keys_in, values_in, allowed, log_total, grad_mix, score_scale):
    soft = jnp.exp(score_block(queries, keys_in, allowed, score_scale) - log_total)
    grad_soft = jnp.einsum("iphe,iqhe->ihpq", grad_mix, values_in, preferred_element_type=F32)
    grad_values = jnp.einsum(
        "ihpq,iphe->iqhe", soft.astype(BF), grad_mix, preferred_element_type=F32
    )
    row_dot = jnp.sum(soft * grad_soft, axis=-1, keepdims=True)
    grad_scores = (soft * (grad_soft - row_dot) * score_scale).astype(BF)
    grad_queries = jnp.einsum("ihpq,iqhe->iphe", grad_scores, keys_in, preferred_element_type=F32)
    grad_keys = jnp.einsum("ihpq,iphe->iqhe", grad_scores, queries, preferred_element_type=F32)
    return (grad_queries.astype(BF), grad_keys, grad_values)


def after(value, *others):
    return lax.optimization_barrier((value, *others))[0]


def follow(value, other):
    return value + (other[(0,) * other.ndim].astype(F32) * 0.0).astype(value.dtype)


def exchange_sum(value):
    for axis in ("wide", "narrow"):
        size = lax.axis_size(axis)
        step = 1
        while step < size:
            value = value + lax.ppermute(value, axis, [(k, k ^ step) for k in range(size)])
            step *= 2
    return value


def body(
    tokens,
    out_grad,
    captions,
    image_blocks,
    caption_owner,
    norm_gains,
    norm_shifts,
    w_query,
    w_key,
    w_value,
    w_out,
    w_cross_query,
    w_cross_key,
    w_cross_value,
    w_cross_out,
    w_up,
    w_down,
):
    scale = HEAD_DIM ** (-0.5)
    n = lax.axis_size("narrow")
    here = lax.axis_index("narrow")
    width = w_query.shape[1]
    heads = width // HEAD_DIM
    part = PIX // CHUNKS
    chunks = [slice(c * part, (c + 1) * part) for c in range(CHUNKS)]
    image_of = (here - jnp.arange(n)) % n

    def relative(blocks):
        return jnp.stack(
            [lax.dynamic_index_in_dim(blocks, image_of[s], 0, False) for s in range(n)]
        )

    def rows_of(*pieces):
        return lax.all_gather(
            jnp.concatenate([p.astype(BF) for p in pieces], axis=1), "wide", axis=0, tiled=True
        )

    def columns_of(piece):
        return lax.all_gather(piece.astype(BF), "wide", axis=1, tiled=True)

    def to_rows(g):
        return lax.psum_scatter(g.astype(BF), "wide", scatter_dimension=0, tiled=True).astype(F32)

    def to_columns(g):
        return lax.psum_scatter(g.astype(BF), "wide", scatter_dimension=1, tiled=True).astype(F32)

    full_qkv = rows_of(w_query, w_key, w_value)
    full_out = columns_of(w_out)
    full_ckv = rows_of(w_cross_key, w_cross_value)
    full_cq = rows_of(w_cross_query)
    full_cout = columns_of(w_cross_out)
    full_up = rows_of(w_up)
    full_down = columns_of(w_down)
    residual0 = tokens.astype(F32)
    xhat1, rstd1 = norm_stats(residual0)
    own1 = (xhat1 * norm_gains[0] + norm_shifts[0]).astype(BF)
    normed1 = spread(own1)
    qkv = product(normed1, full_qkv).astype(BF)
    heads_of = lambda x: x.reshape(x.shape[:-1] + (x.shape[-1] // HEAD_DIM, HEAD_DIM))
    self_q, self_k, self_v = [heads_of(qkv[..., k * width : (k + 1) * width]) for k in range(3)]
    blocks = image_blocks[image_of]
    self_allowed = blocks[:, :, None] == blocks[:, None, :]
    self_mix, self_total = attend(self_q, self_k, self_v, self_allowed, scale)
    self_mix = self_mix.reshape(n, PIX, width)
    text_rows = lax.all_gather(captions, "narrow", axis=0, tiled=True)
    text_count, text_width = text_rows.shape
    ckv = product(text_rows, full_ckv).astype(BF)
    cross_k = heads_of(ckv[None, :, :width])
    cross_v = heads_of(ckv[None, :, width:])
    owner = caption_owner[0]
    part_image = jnp.repeat(image_of, part)
    cross_allowed = (part_image[:, None] == owner[None, :])[None]
    state = []
    for rows in chunks:
        residual1 = residual0[rows] + sink(product(self_mix[:, rows], full_out).astype(BF))
        xhat2, rstd2 = norm_stats(residual1)
        state.append((residual1, xhat2, rstd2))
    normed2 = [spread((s[1] * norm_gains[1] + norm_shifts[1]).astype(BF)) for s in state]
    grad_all = relative(lax.all_gather(out_grad, "narrow", axis=0))
    cross_q, cross_mix, cross_total, state3 = ([], [], [], [])
    for c in range(CHUNKS):
        q = heads_of(product(normed2[c], full_cq).astype(BF).reshape(1, n * part, width))
        mix, total = attend(q, cross_k, cross_v, cross_allowed, scale)
        mix = mix.reshape(n, part, width)
        residual2 = state[c][0] + sink(product(mix, full_cout).astype(BF))
        xhat3, rstd3 = norm_stats(residual2)
        cross_q.append(q)
        cross_mix.append(mix)
        cross_total.append(total)
        state3.append((residual2, xhat3, rstd3))
    normed3 = [spread((s[1] * norm_gains[2] + norm_shifts[2]).astype(BF)) for s in state3]
    out_parts, acts, grad_hiddens, grad2, sums3 = ([], [], [], [], [])
    for c, rows in enumerate(chunks):
        if c > 0:
            normed3[c] = follow(normed3[c], sent)
        hidden = product(normed3[c], full_up)
        grad_rows = grad_all[:, rows]
        acted, gelu_back = jax.vjp(jax.nn.gelu, hidden)
        acted = acted.astype(BF)
        grad_hidden = gelu_back(right_inner(grad_rows, full_down))[0].astype(BF)
        acts.append(acted)
        grad_hiddens.append(grad_hidden)
        sent = lax.optimization_barrier(right_inner(grad_hidden, full_up).astype(BF))
        grad_n3 = sink(sent)
        residual2, xhat3, rstd3 = state3[c]
        sums3.append(norm_sums(grad_n3, xhat3))
        grad2.append(out_grad[rows].astype(F32) + norm_back(grad_n3, xhat3, rstd3, norm_gains[2]))
        out_parts.append(product(acted, full_down).astype(BF))
    cat = lambda xs: jnp.concatenate(xs, axis=1)
    acted, grad_hidden, n3 = (cat(acts), cat(grad_hiddens), cat(normed3))
    grad_down = left_inner(acted, cat([grad_all[:, rows] for rows in chunks]))
    grad_up = left_inner(n3, grad_hidden)
    out_sum = lax.psum_scatter(relative(cat(out_parts)), "narrow", scatter_dimension=0)
    block_out = (jnp.concatenate([s[0] for s in state3]) + out_sum.astype(F32)).astype(BF)
    e2 = [spread(g.astype(BF)) for g in grad2]
    own_down = to_columns(grad_down)
    own_up = to_rows(grad_up)
    e2[-1] = after(e2[-1], grad_down, grad_up)
    grad1, sums2, grad_cqs, grad_ck, grad_cv = ([], [], [], 0.0, 0.0)
    for c in range(CHUNKS):
        grad_mix = heads_of(right_inner(e2[c], full_cout).astype(BF).reshape(1, n * part, width))
        gq, gk, gv = attend_back(
            cross_q[c], cross_k, cross_v, cross_allowed, cross_total[c], grad_mix, scale
        )
        gq = gq.reshape(n, part, width)
        grad_cqs.append(gq)
        grad_ck = grad_ck + gk
        grad_cv = grad_cv + gv
        grad_n2 = sink(right_inner(gq, full_cq).astype(BF))
        _, xhat2, rstd2 = state[c]
        sums2.append(norm_sums(grad_n2, xhat2))
        grad1.append(grad2[c] + norm_back(grad_n2, xhat2, rstd2, norm_gains[1]))
    grad_cout = left_inner(cat(cross_mix), cat(e2))
    grad_cq = left_inner(cat(normed2), cat(grad_cqs))
    grad_ckv = jnp.concatenate(
        [grad_ck.reshape(text_count, width), grad_cv.reshape(text_count, width)], axis=1
    ).astype(BF)
    grad_text_part = right_inner(grad_ckv, full_ckv).astype(BF).reshape(n, -1, text_width)
    grad_wckv = left_inner(text_rows, grad_ckv)
    e1 = [spread(g.astype(BF)) for g in grad1]
    own_cout = to_columns(grad_cout)
    own_cq = to_rows(grad_cq)
    own_ckv = to_rows(grad_wckv)
    e1[-1] = after(e1[-1], grad_cout, grad_cq, grad_wckv, grad_text_part)
    grad_mix = heads_of(cat([right_inner(e, full_out).astype(BF) for e in e1]))
    grad_mix = after(grad_mix, own_down, own_up)
    gq, gk, gv = attend_back(self_q, self_k, self_v, self_allowed, self_total, grad_mix, scale)
    grad_qkv = jnp.concatenate([g.astype(BF).reshape(n, PIX, width) for g in (gq, gk, gv)], axis=-1)
    grad_out = left_inner(self_mix, cat(e1))
    grad_wqkv = left_inner(normed1, grad_qkv)
    grad_n1 = sink(right_inner(after(grad_qkv, grad_wqkv), full_qkv).astype(BF))
    grad_text = sink(relative(after(grad_text_part, grad_mix))).astype(BF)
    grad1 = jnp.concatenate(grad1)
    grad_n1 = after(grad_n1, own_cout, own_cq, own_ckv)
    grad_tokens = (grad1 + norm_back(grad_n1, xhat1, rstd1, norm_gains[0])).astype(BF)
    sums = exchange_sum(jnp.stack([norm_sums(grad_n1, xhat1), sum(sums2), sum(sums3)]))
    own_out = to_columns(grad_out)
    own_qkv = to_rows(grad_wqkv)
    return (
        block_out,
        grad_tokens,
        grad_text,
        sums[:, 0],
        sums[:, 1],
        own_qkv[:, :width],
        own_qkv[:, width : 2 * width],
        own_qkv[:, 2 * width :],
        own_out,
        own_cq,
        own_ckv[:, :width],
        own_ckv[:, width:],
        own_cout,
        own_up,
        own_down,
    )


def solution(mesh):
    in_specs = (
        P(("wide", "narrow"), None),
        P(("wide", "narrow"), None),
        P(("wide", "narrow"), None),
        P("wide", None),
        P("wide", None),
        P(),
        P(),
        P("wide", "narrow"),
        P("wide", "narrow"),
        P("wide", "narrow"),
        P("narrow", "wide"),
        P("wide", "narrow"),
        P("wide", "narrow"),
        P("wide", "narrow"),
        P("narrow", "wide"),
        P("wide", "narrow"),
        P("narrow", "wide"),
    )
    out_specs = (
        P(("wide", "narrow"), None),
        P(("wide", "narrow"), None),
        P(("wide", "narrow"), None),
        P(),
        P(),
        P("wide", "narrow"),
        P("wide", "narrow"),
        P("wide", "narrow"),
        P("narrow", "wide"),
        P("wide", "narrow"),
        P("wide", "narrow"),
        P("wide", "narrow"),
        P("narrow", "wide"),
        P("wide", "narrow"),
        P("narrow", "wide"),
    )
    return jax.shard_map(body, mesh=mesh, in_specs=in_specs, out_specs=out_specs, check_vma=False)
```

profile of v0, /device:TPU:0, one launch (start us, length us, event | category | flops | bytes accessed | tf_op | source)
XLA Modules:
  0.0 1377.7 jit_solution(2369147938922174307)
XLA Ops:
  28.0 21.0 %collective-permute-done = bf16[256,2048]{1,0:T(8,128)(2,1)S(1)} collective-permute-done((bf16[256,2048]{1,0:T(8,128)(2,1)S(1)}, bf16[256,2048]{1,0:T(8,128)(2,1)S(1)}, u32[]{:S(2)}, u32[]{:S(2)}) %collective-permute-start) | collective-permute-done | bytes 1048608 | tf_op jit(solution)/shard_map/ppermute | solution.py:39
  57.5 22.6 %collective-permute-done.2 = bf16[256,2048]{1,0:T(8,128)(2,1)} collective-permute-done((bf16[256,2048]{1,0:T(8,128)(2,1)S(1)}, bf16[256,2048]{1,0:T(8,128)(2,1)}, u32[]{:S(2)}, u32[]{:S(2)}) %collective-permute-start.2) | collective-permute-done | bytes 1048608 | tf_op jit(solution)/shard_map/ppermute | solution.py:40
  85.7 19.9 %collective-permute-done.3 = bf16[256,2048]{1,0:T(8,128)(2,1)S(1)} collective-permute-done((bf16[256,2048]{1,0:T(8,128)(2,1)}, bf16[256,2048]{1,0:T(8,128)(2,1)S(1)}, u32[]{:S(2)}, u32[]{:S(2)}) %collective-permute-start.3) | collective-permute-done | bytes 1048608 | tf_op jit(solution)/shard_map/ppermute | solution.py:40
  106.6 9.4 fusion.91
  133.5 18.8 %collective-permute-done.6 = bf16[128,2048]{1,0:T(8,128)(2,1)S(1)} collective-permute-done((bf16[128,2048]{1,0:T(8,128)(2,1)S(1)}, bf16[128,2048]{1,0:T(8,128)(2,1)S(1)}, u32[]{:S(2)}, u32[]{:S(2)}) %collective-permute-start.6) | collective-permute-done | bytes 524320 | tf_op jit(solution)/shard_map/ppermute | solution.py:53
  157.7 17.1 %collective-permute-done.24 = bf16[128,2048]{1,0:T(8,128)(2,1)S(1)} collective-permute-done((bf16[128,2048]{1,0:T(8,128)(2,1)S(1)}, bf16[128,2048]{1,0:T(8,128)(2,1)S(1)}, u32[]{:S(2)}, u32[]{:S(2)}) %collective-permute-start.24) | collective-permute-done | bytes 524320 | tf_op jit(solution)/shard_map/ppermute | solution.py:53
  180.2 17.0 %collective-permute-done.7 = bf16[128,2048]{1,0:T(8,128)(2,1)S(1)} collective-permute-done((bf16[128,2048]{1,0:T(8,128)(2,1)S(1)}, bf16[128,2048]{1,0:T(8,128)(2,1)S(1)}, u32[]{:S(2)}, u32[]{:S(2)}) %collective-permute-start.7) | collective-permute-done | bytes 524320 | tf_op jit(solution)/shard_map/ppermute | solution.py:53
  203.4 16.4 %collective-permute-done.25 = bf16[128,2048]{1,0:T(8,128)(2,1)S(1)} collective-permute-done((bf16[128,2048]{1,0:T(8,128)(2,1)S(1)}, bf16[128,2048]{1,0:T(8,128)(2,1)S(1)}, u32[]{:S(2)}, u32[]{:S(2)}) %collective-permute-start.25) | collective-permute-done | bytes 524320 | tf_op jit(solution)/shard_map/ppermute | solution.py:53
  226.3 15.9 %collective-permute-done.8 = bf16[128,2048]{1,0:T(8,128)(2,1)S(1)} collective-permute-done((bf16[128,2048]{1,0:T(8,128)(2,1)S(1)}, bf16[128,2048]{1,0:T(8,128)(2,1)S(1)}, u32[]{:S(2)}, u32[]{:S(2)}) %collective-permute-start.8) | collective-permute-done | bytes 524320 | tf_op jit(solution)/shard_map/ppermute | solution.py:53
  242.2 19.3 %collective-permute-done.26 = bf16[128,2048]{1,0:T(8,128)(2,1)S(1)} collective-permute-done((bf16[128,2048]{1,0:T(8,128)(2,1)S(1)}, bf16[128,2048]{1,0:T(8,128)(2,1)S(1)}, u32[]{:S(2)}, u32[]{:S(2)}) %collective-permute-start.26) | collective-permute-done | bytes 524320 | tf_op jit(solution)/shard_map/ppermute | solution.py:53
  282.2 9.1 collective-permute-done.31
  294.3 8.2 collective-permute-done.14
  304.8 9.1 collective-permute-done.32
  338.4 9.5 fusion.222
  373.6 19.3 %collective-permute-done.18 = bf16[128,2048]{1,0:T(8,128)(2,1)S(1)} collective-permute-done((bf16[128,2048]{1,0:T(8,128)(2,1)S(1)}, bf16[128,2048]{1,0:T(8,128)(2,1)S(1)}, u32[]{:S(2)}, u32[]{:S(2)}) %collective-permute-start.18) | collective-permute-done | bytes 524320 | tf_op jit(solution)/shard_map/ppermute | solution.py:53
  398.4 17.0 %collective-permute-done.36 = bf16[128,2048]{1,0:T(8,128)(2,1)S(1)} collective-permute-done((bf16[128,2048]{1,0:T(8,128)(2,1)S(1)}, bf16[128,2048]{1,0:T(8,128)(2,1)S(1)}, u32[]{:S(2)}, u32[]{:S(2)}) %collective-permute-start.36) | collective-permute-done | bytes 524320 | tf_op jit(solution)/shard_map/ppermute | solution.py:53
  420.8 17.0 %collective-permute-done.19 = bf16[128,2048]{1,0:T(8,128)(2,1)S(1)} collective-permute-done((bf16[128,2048]{1,0:T(8,128)(2,1)S(1)}, bf16[128,2048]{1,0:T(8,128)(2,1)S(1)}, u32[]{:S(2)}, u32[]{:S(2)}) %collective-permute-start.19) | collective-permute-done | bytes 524320 | tf_op jit(solution)/shard_map/ppermute | solution.py:53
  444.0 16.4 %collective-permute-done.37 = bf16[128,2048]{1,0:T(8,128)(2,1)S(1)} collective-permute-done((bf16[128,2048]{1,0:T(8,128)(2,1)S(1)}, bf16[128,2048]{1,0:T(8,128)(2,1)S(1)}, u32[]{:S(2)}, u32[]{:S(2)}) %collective-permute-start.37) | collective-permute-done | bytes 524320 | tf_op jit(solution)/shard_map/ppermute | solution.py:53
  466.4 15.7 %collective-permute-done.20 = bf16[128,2048]{1,0:T(8,128)(2,1)S(1)} collective-permute-done((bf16[128,2048]{1,0:T(8,128)(2,1)S(1)}, bf16[128,2048]{1,0:T(8,128)(2,1)S(1)}, u32[]{:S(2)}, u32[]{:S(2)}) %collective-permute-start.20) | collective-permute-done | bytes 524320 | tf_op jit(solution)/shard_map/ppermute | solution.py:53
  482.8 14.0 %collective-permute-done.38 = bf16[128,2048]{1,0:T(8,128)(2,1)S(1)} collective-permute-done((bf16[128,2048]{1,0:T(8,128)(2,1)S(1)}, bf16[128,2048]{1,0:T(8,128)(2,1)S(1)}, u32[]{:S(2)}, u32[]{:S(2)}) %collective-permute-start.38) | collective-permute-done | bytes 524320 | tf_op jit(solution)/shard_map/ppermute | solution.py:53
  500.0 5.8 collective-permute-start.48
  507.2 7.0 collective-permute-start.42
  532.0 7.0 collective-permute-done.50
  540.2 9.5 collective-permute-done.44
  563.9 11.9 multiply_convert_fusion.4
  575.8 32.7 %all-gather.25.cloned.1.call-done = bf16[2048,2048]{1,0:T(8,128)(2,1)} async-done(((bf16[2048,256]{1,0:T(8,128)(2,1)}), bf16[2048,2048]{1,0:T(8,128)(2,1)}) %all-gather.25.cloned.1.call-update) | async-done | bytes 8388624 | tf_op jit(solution)/shard_map/all_gather | solution.py:160
  608.5 10.5 fusion.29
  627.7 10.1 multiply_convert_fusion.3
  637.9 8.3 fusion.36
  646.2 13.5 convolution_bitcast_fusion.2
  659.7 14.4 %convolution_bitcast_fusion.3 = bf16[2048,2048]{1,0:T(8,128)(2,1)} fusion(bf16[4,128,2048]{2,1,0:T(8,128)(2,1)} %get-tuple-element.189, bf16[4,128,2048]{2,1,0:T(8,128)(2,1)} %get-tuple-element.187, bf16[1,256,2048]{2,1,0:T(8,128)(2,1)} %copy-done.45, bf16[1,256,2048]{2,1,0:T(8,128)(2,1)} %copy-done.46, bf16[1,256,2048]{2,1,0:T(8,128)(2,1)} %copy-done.47, ...), kind=kOutput, calls=%fused_computation.7 | convolution fusion | flops 8604614656 | bytes 16777216 | tf_op jit(solution)/shard_map/dot_general | solution.py:29
  680.0 8.5 fusion.117
  736.0 10.8 collective-permute-done.74
  769.6 9.9 collective-permute-done.79
  782.6 8.2 collective-permute-done.62
  792.1 9.9 collective-permute-done.80
  804.9 18.6 %collective-permute-done.81 = bf16[128,2048]{1,0:T(8,128)(2,1)S(1)} collective-permute-done((bf16[128,2048]{1,0:T(8,128)(2,1)S(1)}, bf16[128,2048]{1,0:T(8,128)(2,1)S(1)}, u32[]{:S(2)}, u32[]{:S(2)}) %collective-permute-start.81) | collective-permute-done | bytes 524320 | tf_op jit(solution)/shard_map/ppermute | solution.py:40
  842.5 9.4 fusion.265
  856.0 9.7 fusion.262
  873.1 8.8 fusion.120
  881.9 8.4 fusion.123
  922.0 8.3 fusion.131
  932.9 10.6 collective-permute-start.85
  947.9 20.0 %collective-permute-start.68 = (bf16[128,2048]{1,0:T(8,128)(2,1)}, bf16[128,2048]{1,0:T(8,128)(2,1)}, u32[]{:S(2)}, u32[]{:S(2)}) collective-permute-start(bf16[128,2048]{1,0:T(8,128)(2,1)} %get-tuple-element.99), channel_id=1, source_target_pairs={{0,1},{1,2},{2,3},{4,5},{5,6},{6,7},{8,9},{9,10},{10,11},{12,13},{... | collective-permute-start | bytes 1572872 | tf_op jit(solution)/shard_map/ppermute | solution.py:53
  969.3 10.3 fusion.226
  981.3 11.5 collective-permute-start.86
  996.2 16.9 %collective-permute-done.86 = bf16[128,2048]{1,0:T(8,128)(2,1)S(1)} collective-permute-done((bf16[128,2048]{1,0:T(8,128)(2,1)S(1)}, bf16[128,2048]{1,0:T(8,128)(2,1)S(1)}, u32[]{:S(2)}, u32[]{:S(2)}) %collective-permute-start.86) | collective-permute-done | bytes 524320 | tf_op jit(solution)/shard_map/ppermute | solution.py:53
  1019.9 25.2 %collective-permute-start.96 = (bf16[128,2048]{1,0:T(8,128)(2,1)S(1)}, bf16[128,2048]{1,0:T(8,128)(2,1)S(1)}, u32[]{:S(2)}, u32[]{:S(2)}) collective-permute-start(bf16[128,2048]{1,0:T(8,128)(2,1)S(1)} %get-tuple-element.68), channel_id=1, source_target_pairs={{0,1},{1,2},{2,3},{4,5},{5,6},{6,7},{8,9},{9,10},{10,11},{12,13},{... | collective-permute-start | bytes 1572872 | tf_op jit(solution)/shard_map/ppermute | solution.py:39
  1051.1 6.7 convolution_bitcast_fusion.1
  1059.8 7.4 collective-permute-done.91
  1069.4 10.2 convolution_convert_fusion
  1088.5 11.1 collective-permute-done.99
  1100.0 6.0 collective-permute-done.93
  1135.6 9.9 fusion.219
  1147.0 9.9 fusion.216
  1161.7 8.9 convolution_bitcast_fusion
  1170.6 10.6 fusion.94
  1189.1 17.9 %collective-permute-done.102 = bf16[256,2048]{1,0:T(8,128)(2,1)S(1)} collective-permute-done((bf16[256,2048]{1,0:T(8,128)(2,1)S(1)}, bf16[256,2048]{1,0:T(8,128)(2,1)S(1)}, u32[]{:S(2)}, u32[]{:S(2)}) %collective-permute-start.102) | collective-permute-done | bytes 1048608 | tf_op jit(solution)/shard_map/ppermute | solution.py:53
  1219.3 10.2 collective-permute-done.108
  1237.7 14.3 %collective-permute-done.103 = bf16[256,2048]{1,0:T(8,128)(2,1)} collective-permute-done((bf16[256,2048]{1,0:T(8,128)(2,1)}, bf16[256,2048]{1,0:T(8,128)(2,1)}, u32[]{:S(2)}, u32[]{:S(2)}) %collective-permute-start.103) | collective-permute-done | bytes 1048608 | tf_op jit(solution)/shard_map/ppermute | solution.py:53
  1266.5 8.0 collective-permute-done.109
  1284.8 12.2 collective-permute-done.104
  1321.9 19.2 %collective-permute-start.118 = (f32[3,2,2048]{2,0,1:T(4,128)S(1)}, f32[3,2,2048]{2,0,1:T(4,128)S(1)}, u32[]{:S(2)}, u32[]{:S(2)}) collective-permute-start(f32[3,2,2048]{2,0,1:T(4,128)S(1)} %add.569), channel_id=1, source_target_pairs={{0,2},{1,3},{2,0},{3,1},{4,6},{5,7},{6,4},{7,5},{8,10},{9,11},{10,... | collective-permute-start | bytes 147464 | tf_op jit(solution)/shard_map/ppermute | solution.py:116
  1344.0 20.7 %collective-permute-done.118 = f32[3,2,2048]{2,0,1:T(4,128)S(1)} collective-permute-done((f32[3,2,2048]{2,0,1:T(4,128)S(1)}, f32[3,2,2048]{2,0,1:T(4,128)S(1)}, u32[]{:S(2)}, u32[]{:S(2)}) %collective-permute-start.118) | collective-permute-done | bytes 49184 | tf_op jit(solution)/shard_map/ppermute | solution.py:116
  (742 shorter events, 520.2 us)
Async XLA Ops:
  7.2 99.4 %all-gather.11.cloned.1.call-start = ((), (), s32[]{:S(2)}) async-start(), calls=%async_computation.8 | async-start | bytes 7077888 | tf_op jit(solution)/shard_map/all_gather | solution.py:155
  11.6 112.8 %all-gather.13.cloned.1.call-start = ((), (), s32[]{:S(2)}) async-start(), calls=%async_computation.9 | async-start | bytes 2359296 | tf_op jit(solution)/shard_map/all_gather | solution.py:160
  12.4 310.2 %all-gather.19.cloned.1.call-start = ((), (), s32[]{:S(2)}) async-start(), calls=%async_computation.12 | async-start | bytes 2359296 | tf_op jit(solution)/shard_map/all_gather | solution.py:155
  13.2 325.2 %all-gather.17.cloned.1.call-start = ((), (), s32[]{:S(2)}) async-start(), calls=%async_computation.11 | async-start | bytes 5242880 | tf_op jit(solution)/shard_map/all_gather | solution.py:186
  13.8 324.6 %all-gather.15.cloned.1.call-start = ((), (), s32[]{:S(2)}) async-start(), calls=%async_computation.10 | async-start | bytes 9437184 | tf_op jit(solution)/shard_map/all_gather | solution.py:155
  16.5 346.2 %all-gather.21.cloned.1.call-start = ((), (), s32[]{:S(2)}) async-start(), calls=%async_computation.13 | async-start | bytes 2359296 | tf_op jit(solution)/shard_map/all_gather | solution.py:160
  18.4 507.8 %all-gather.27.cloned.1.call-start = ((), (), s32[]{:S(2)}) async-start(), calls=%async_computation.24 | async-start | bytes 5242880 | tf_op jit(solution)/shard_map/all_gather | solution.py:200
  19.2 544.7 %all-gather.23.cloned.1.call-start = ((), (), s32[]{:S(2)}) async-start(), calls=%async_computation.14 | async-start | bytes 9437184 | tf_op jit(solution)/shard_map/all_gather | solution.py:155
  20.4 588.1 %all-gather.25.cloned.1.call-start = ((), (), s32[]{:S(2)}) async-start(), calls=%async_computation.15 | async-start | bytes 9437184 | tf_op jit(solution)/shard_map/all_gather | solution.py:160
  21.7 27.4 %collective-permute-start = (bf16[256,2048]{1,0:T(8,128)(2,1)S(1)}, bf16[256,2048]{1,0:T(8,128)(2,1)S(1)}, u32[]{:S(2)}, u32[]{:S(2)}) collective-permute-start(bf16[256,2048]{1,0:T(8,128)(2,1)S(1)} %add_convert_fusion.4), channel_id=1, source_target_pairs={{0,1},{1,2},{2,3},{4,5},{5,6},{6,7},{8,9},{9,10},{10,11},{12,13},{... | collective-permute-start | bytes 3145736 | tf_op jit(solution)/shard_map/ppermute | solution.py:39
  26.7 26.5 %collective-permute-start.1 = (bf16[256,2048]{1,0:T(8,128)(2,1)S(1)}, bf16[256,2048]{1,0:T(8,128)(2,1)S(1)}, u32[]{:S(2)}, u32[]{:S(2)}) collective-permute-start(bf16[256,2048]{1,0:T(8,128)(2,1)S(1)} %add_convert_fusion.4), channel_id=1, source_target_pairs={{1,0},{2,1},{3,2},{5,4},{6,5},{7,6},{9,8},{10,9},{11,10},{13,12},{... | collective-permute-start | bytes 3145736 | tf_op jit(solution)/shard_map/ppermute | solution.py:40
  53.2 26.9 %collective-permute-start.2 = (bf16[256,2048]{1,0:T(8,128)(2,1)S(1)}, bf16[256,2048]{1,0:T(8,128)(2,1)}, u32[]{:S(2)}, u32[]{:S(2)}) collective-permute-start(bf16[256,2048]{1,0:T(8,128)(2,1)S(1)} %collective-permute-done.1), channel_id=1, source_target_pairs={{1,0},{2,1},{5,4},{6,5},{9,8},{10,9},{13,12},{14,13},{17,16},{18,1... | collective-permute-start | bytes 3145736 | tf_op jit(solution)/shard_map/ppermute | solution.py:40
  55.2 27.8 %collective-permute-start.5 = (bf16[256,2048]{1,0:T(8,128)(2,1)}, bf16[256,2048]{1,0:T(8,128)(2,1)}, u32[]{:S(2)}, u32[]{:S(2)}) collective-permute-start(bf16[256,2048]{1,0:T(8,128)(2,1)} %collective-permute-done.4), channel_id=1, source_target_pairs={{2,3},{6,7},{10,11},{14,15},{18,19},{22,23},{26,27},{30,31}} | collective-permute-start | bytes 3145736 | tf_op jit(solution)/shard_map/ppermute | solution.py:39
  131.5 43.3 %collective-permute-start.24 = (bf16[128,2048]{1,0:T(8,128)(2,1)S(1)}, bf16[128,2048]{1,0:T(8,128)(2,1)S(1)}, u32[]{:S(2)}, u32[]{:S(2)}) collective-permute-start(bf16[128,2048]{1,0:T(8,128)(2,1)S(1)} %get-tuple-element.147), channel_id=1, source_target_pairs={{0,1},{4,5},{8,9},{12,13},{16,17},{20,21},{24,25},{28,29}} | collective-permute-start | bytes 1572872 | tf_op jit(solution)/shard_map/ppermute | solution.py:53
  132.8 42.0 %collective-permute-start.27 = (bf16[128,2048]{1,0:T(8,128)(2,1)S(1)}, bf16[128,2048]{1,0:T(8,128)(2,1)S(1)}, u32[]{:S(2)}, u32[]{:S(2)}) collective-permute-start(bf16[128,2048]{1,0:T(8,128)(2,1)S(1)} %get-tuple-element.148), channel_id=1, source_target_pairs={{3,2},{7,6},{11,10},{15,14},{19,18},{23,22},{27,26},{31,30}} | collective-permute-start | bytes 1572872 | tf_op jit(solution)/shard_map/ppermute | solution.py:54
  152.6 44.7 %collective-permute-start.7 = (bf16[128,2048]{1,0:T(8,128)(2,1)S(1)}, bf16[128,2048]{1,0:T(8,128)(2,1)S(1)}, u32[]{:S(2)}, u32[]{:S(2)}) collective-permute-start(bf16[128,2048]{1,0:T(8,128)(2,1)S(1)} %get-tuple-element.139), channel_id=1, source_target_pairs={{0,1},{1,2},{4,5},{5,6},{8,9},{9,10},{12,13},{13,14},{16,17},{17,1... | collective-permute-start | bytes 1572872 | tf_op jit(solution)/shard_map/ppermute | solution.py:53
  157.0 40.2 %collective-permute-start.10 = (bf16[128,2048]{1,0:T(8,128)(2,1)S(1)}, bf16[128,2048]{1,0:T(8,128)(2,1)S(1)}, u32[]{:S(2)}, u32[]{:S(2)}) collective-permute-start(bf16[128,2048]{1,0:T(8,128)(2,1)S(1)} %get-tuple-element.140), channel_id=1, source_target_pairs={{2,1},{3,2},{6,5},{7,6},{10,9},{11,10},{14,13},{15,14},{18,17},{19... | collective-permute-start | bytes 1572872 | tf_op jit(solution)/shard_map/ppermute | solution.py:54
  175.1 44.6 %collective-permute-start.25 = (bf16[128,2048]{1,0:T(8,128)(2,1)S(1)}, bf16[128,2048]{1,0:T(8,128)(2,1)S(1)}, u32[]{:S(2)}, u32[]{:S(2)}) collective-permute-start(bf16[128,2048]{1,0:T(8,128)(2,1)S(1)} %get-tuple-element.145), channel_id=1, source_target_pairs={{0,1},{1,2},{4,5},{5,6},{8,9},{9,10},{12,13},{13,14},{16,17},{17,1... | collective-permute-start | bytes 1572872 | tf_op jit(solution)/shard_map/ppermute | solution.py:53
  179.5 40.2 %collective-permute-start.28 = (bf16[128,2048]{1,0:T(8,128)(2,1)S(1)}, bf16[128,2048]{1,0:T(8,128)(2,1)S(1)}, u32[]{:S(2)}, u32[]{:S(2)}) collective-permute-start(bf16[128,2048]{1,0:T(8,128)(2,1)S(1)} %get-tuple-element.146), channel_id=1, source_target_pairs={{2,1},{3,2},{6,5},{7,6},{10,9},{11,10},{14,13},{15,14},{18,17},{19... | collective-permute-start | bytes 1572872 | tf_op jit(solution)/shard_map/ppermute | solution.py:54
  197.7 44.5 %collective-permute-start.8 = (bf16[128,2048]{1,0:T(8,128)(2,1)S(1)}, bf16[128,2048]{1,0:T(8,128)(2,1)S(1)}, u32[]{:S(2)}, u32[]{:S(2)}) collective-permute-start(bf16[128,2048]{1,0:T(8,128)(2,1)S(1)} %get-tuple-element.137), channel_id=1, source_target_pairs={{0,1},{1,2},{2,3},{4,5},{5,6},{6,7},{8,9},{9,10},{10,11},{12,13},{... | collective-permute-start | bytes 1572872 | tf_op jit(solution)/shard_map/ppermute | solution.py:53
  202.1 40.1 %collective-permute-start.11 = (bf16[128,2048]{1,0:T(8,128)(2,1)S(1)}, bf16[128,2048]{1,0:T(8,128)(2,1)S(1)}, u32[]{:S(2)}, u32[]{:S(2)}) collective-permute-start(bf16[128,2048]{1,0:T(8,128)(2,1)S(1)} %get-tuple-element.138), channel_id=1, source_target_pairs={{1,0},{2,1},{3,2},{5,4},{6,5},{7,6},{9,8},{10,9},{11,10},{13,12},{... | collective-permute-start | bytes 1572872 | tf_op jit(solution)/shard_map/ppermute | solution.py:54
  220.1 41.4 %collective-permute-start.26 = (bf16[128,2048]{1,0:T(8,128)(2,1)S(1)}, bf16[128,2048]{1,0:T(8,128)(2,1)S(1)}, u32[]{:S(2)}, u32[]{:S(2)}) collective-permute-start(bf16[128,2048]{1,0:T(8,128)(2,1)S(1)} %get-tuple-element.143), channel_id=1, source_target_pairs={{0,1},{1,2},{2,3},{4,5},{5,6},{6,7},{8,9},{9,10},{10,11},{12,13},{... | collective-permute-start | bytes 1572872 | tf_op jit(solution)/shard_map/ppermute | solution.py:53
  224.8 36.8 %collective-permute-start.29 = (bf16[128,2048]{1,0:T(8,128)(2,1)S(1)}, bf16[128,2048]{1,0:T(8,128)(2,1)S(1)}, u32[]{:S(2)}, u32[]{:S(2)}) collective-permute-start(bf16[128,2048]{1,0:T(8,128)(2,1)S(1)} %get-tuple-element.144), channel_id=1, source_target_pairs={{1,0},{2,1},{3,2},{5,4},{6,5},{7,6},{9,8},{10,9},{11,10},{13,12},{... | collective-permute-start | bytes 1572872 | tf_op jit(solution)/shard_map/ppermute | solution.py:54
  279.0 839.9 %reduce-scatter.13.cloned.1.call-start = ((), (), s32[]{:S(2)}) async-start(), calls=%async_computation.18 | async-start | bytes 9437184 | tf_op jit(solution)/shard_map/reduce_scatter | solution.py:163
  366.1 26.9 %collective-permute-start.18 = (bf16[128,2048]{1,0:T(8,128)(2,1)S(1)}, bf16[128,2048]{1,0:T(8,128)(2,1)S(1)}, u32[]{:S(2)}, u32[]{:S(2)}) collective-permute-start(bf16[128,2048]{1,0:T(8,128)(2,1)S(1)} %get-tuple-element.127), channel_id=1, source_target_pairs={{0,1},{4,5},{8,9},{12,13},{16,17},{20,21},{24,25},{28,29}} | collective-permute-start | bytes 1572872 | tf_op jit(solution)/shard_map/ppermute | solution.py:53
  371.6 43.8 %collective-permute-start.36 = (bf16[128,2048]{1,0:T(8,128)(2,1)S(1)}, bf16[128,2048]{1,0:T(8,128)(2,1)S(1)}, u32[]{:S(2)}, u32[]{:S(2)}) collective-permute-start(bf16[128,2048]{1,0:T(8,128)(2,1)S(1)} %get-tuple-element.133), channel_id=1, source_target_pairs={{0,1},{4,5},{8,9},{12,13},{16,17},{20,21},{24,25},{28,29}} | collective-permute-start | bytes 1572872 | tf_op jit(solution)/shard_map/ppermute | solution.py:53
  372.9 42.5 %collective-permute-start.39 = (bf16[128,2048]{1,0:T(8,128)(2,1)S(1)}, bf16[128,2048]{1,0:T(8,128)(2,1)S(1)}, u32[]{:S(2)}, u32[]{:S(2)}) collective-permute-start(bf16[128,2048]{1,0:T(8,128)(2,1)S(1)} %get-tuple-element.134), channel_id=1, source_target_pairs={{3,2},{7,6},{11,10},{15,14},{19,18},{23,22},{27,26},{31,30}} | collective-permute-start | bytes 1572872 | tf_op jit(solution)/shard_map/ppermute | solution.py:54
  393.2 44.6 %collective-permute-start.19 = (bf16[128,2048]{1,0:T(8,128)(2,1)S(1)}, bf16[128,2048]{1,0:T(8,128)(2,1)S(1)}, u32[]{:S(2)}, u32[]{:S(2)}) collective-permute-start(bf16[128,2048]{1,0:T(8,128)(2,1)S(1)} %get-tuple-element.125), channel_id=1, source_target_pairs={{0,1},{1,2},{4,5},{5,6},{8,9},{9,10},{12,13},{13,14},{16,17},{17,1... | collective-permute-start | bytes 1572872 | tf_op jit(solution)/shard_map/ppermute | solution.py:53
  397.7 40.2 %collective-permute-start.22 = (bf16[128,2048]{1,0:T(8,128)(2,1)S(1)}, bf16[128,2048]{1,0:T(8,128)(2,1)S(1)}, u32[]{:S(2)}, u32[]{:S(2)}) collective-permute-start(bf16[128,2048]{1,0:T(8,128)(2,1)S(1)} %get-tuple-element.126), channel_id=1, source_target_pairs={{2,1},{3,2},{6,5},{7,6},{10,9},{11,10},{14,13},{15,14},{18,17},{19... | collective-permute-start | bytes 1572872 | tf_op jit(solution)/shard_map/ppermute | solution.py:54
  415.7 44.6 %collective-permute-start.37 = (bf16[128,2048]{1,0:T(8,128)(2,1)S(1)}, bf16[128,2048]{1,0:T(8,128)(2,1)S(1)}, u32[]{:S(2)}, u32[]{:S(2)}) collective-permute-start(bf16[128,2048]{1,0:T(8,128)(2,1)S(1)} %get-tuple-element.131), channel_id=1, source_target_pairs={{0,1},{1,2},{4,5},{5,6},{8,9},{9,10},{12,13},{13,14},{16,17},{17,1... | collective-permute-start | bytes 1572872 | tf_op jit(solution)/shard_map/ppermute | solution.py:53
  420.1 40.2 %collective-permute-start.40 = (bf16[128,2048]{1,0:T(8,128)(2,1)S(1)}, bf16[128,2048]{1,0:T(8,128)(2,1)S(1)}, u32[]{:S(2)}, u32[]{:S(2)}) collective-permute-start(bf16[128,2048]{1,0:T(8,128)(2,1)S(1)} %get-tuple-element.132), channel_id=1, source_target_pairs={{2,1},{3,2},{6,5},{7,6},{10,9},{11,10},{14,13},{15,14},{18,17},{19... | collective-permute-start | bytes 1572872 | tf_op jit(solution)/shard_map/ppermute | solution.py:54
  438.2 43.9 %collective-permute-start.20 = (bf16[128,2048]{1,0:T(8,128)(2,1)S(1)}, bf16[128,2048]{1,0:T(8,128)(2,1)S(1)}, u32[]{:S(2)}, u32[]{:S(2)}) collective-permute-start(bf16[128,2048]{1,0:T(8,128)(2,1)S(1)} %get-tuple-element.123), channel_id=1, source_target_pairs={{0,1},{1,2},{2,3},{4,5},{5,6},{6,7},{8,9},{9,10},{10,11},{12,13},{... | collective-permute-start | bytes 1572872 | tf_op jit(solution)/shard_map/ppermute | solution.py:53
  442.7 39.5 %collective-permute-start.23 = (bf16[128,2048]{1,0:T(8,128)(2,1)S(1)}, bf16[128,2048]{1,0:T(8,128)(2,1)S(1)}, u32[]{:S(2)}, u32[]{:S(2)}) collective-permute-start(bf16[128,2048]{1,0:T(8,128)(2,1)S(1)} %get-tuple-element.124), channel_id=1, source_target_pairs={{1,0},{2,1},{3,2},{5,4},{6,5},{7,6},{9,8},{10,9},{11,10},{13,12},{... | collective-permute-start | bytes 1572872 | tf_op jit(solution)/shard_map/ppermute | solution.py:54
  460.7 36.2 %collective-permute-start.38 = (bf16[128,2048]{1,0:T(8,128)(2,1)S(1)}, bf16[128,2048]{1,0:T(8,128)(2,1)S(1)}, u32[]{:S(2)}, u32[]{:S(2)}) collective-permute-start(bf16[128,2048]{1,0:T(8,128)(2,1)S(1)} %get-tuple-element.129), channel_id=1, source_target_pairs={{0,1},{1,2},{2,3},{4,5},{5,6},{6,7},{8,9},{9,10},{10,11},{12,13},{... | collective-permute-start | bytes 1572872 | tf_op jit(solution)/shard_map/ppermute | solution.py:53
  465.1 31.7 %collective-permute-start.41 = (bf16[128,2048]{1,0:T(8,128)(2,1)S(1)}, bf16[128,2048]{1,0:T(8,128)(2,1)S(1)}, u32[]{:S(2)}, u32[]{:S(2)}) collective-permute-start(bf16[128,2048]{1,0:T(8,128)(2,1)S(1)} %get-tuple-element.130), channel_id=1, source_target_pairs={{1,0},{2,1},{3,2},{5,4},{6,5},{7,6},{9,8},{10,9},{11,10},{13,12},{... | collective-permute-start | bytes 1572872 | tf_op jit(solution)/shard_map/ppermute | solution.py:54
  523.2 27.8 %collective-permute-start.52 = (bf16[128,2048]{1,0:T(8,128)(2,1)}, bf16[128,2048]{1,0:T(8,128)(2,1)}, u32[]{:S(2)}, u32[]{:S(2)}) collective-permute-start(bf16[128,2048]{1,0:T(8,128)(2,1)} %collective-permute-done.48), channel_id=1, source_target_pairs={{1,2},{2,3},{5,6},{6,7},{9,10},{10,11},{13,14},{14,15},{17,18},{18... | collective-permute-start | bytes 1572872 | tf_op jit(solution)/shard_map/ppermute | solution.py:39
  538.9 86.1 %collective-permute-start.51 = (bf16[128,2048]{1,0:T(8,128)(2,1)}, bf16[128,2048]{1,0:T(8,128)(2,1)}, u32[]{:S(2)}, u32[]{:S(2)}) collective-permute-start(bf16[128,2048]{1,0:T(8,128)(2,1)} %collective-permute-done.50), channel_id=1, source_target_pairs={{1,0},{5,4},{9,8},{13,12},{17,16},{21,20},{25,24},{29,28}} | collective-permute-start | bytes 1572872 | tf_op jit(solution)/shard_map/ppermute | solution.py:40
  552.9 73.3 %collective-permute-start.53 = (bf16[128,2048]{1,0:T(8,128)(2,1)}, bf16[128,2048]{1,0:T(8,128)(2,1)}, u32[]{:S(2)}, u32[]{:S(2)}) collective-permute-start(bf16[128,2048]{1,0:T(8,128)(2,1)} %collective-permute-done.52), channel_id=1, source_target_pairs={{2,3},{6,7},{10,11},{14,15},{18,19},{22,23},{26,27},{30,31}} | collective-permute-start | bytes 1572872 | tf_op jit(solution)/shard_map/ppermute | solution.py:39
  659.7 462.1 %reduce-scatter.11.cloned.1.call-start = ((), (), s32[]{:S(2)}) async-start(), calls=%async_computation.17 | async-start | bytes 9437184 | tf_op jit(solution)/shard_map/reduce_scatter | solution.py:166
  674.2 541.5 %reduce-scatter.15.cloned.1.call-start = ((), (), s32[]{:S(2)}) async-start(), calls=%async_computation.19 | async-start | bytes 2359296 | tf_op jit(solution)/shard_map/reduce_scatter | solution.py:166
  752.5 27.1 %collective-permute-start.79 = (bf16[128,2048]{1,0:T(8,128)(2,1)S(1)}, bf16[128,2048]{1,0:T(8,128)(2,1)S(1)}, u32[]{:S(2)}, u32[]{:S(2)}) collective-permute-start(bf16[128,2048]{1,0:T(8,128)(2,1)S(1)} %get-tuple-element.149), channel_id=1, source_target_pairs={{1,0},{2,1},{3,2},{5,4},{6,5},{7,6},{9,8},{10,9},{11,10},{13,12},{... | collective-permute-start | bytes 1572872 | tf_op jit(solution)/shard_map/ppermute | solution.py:40
  753.8 27.1 %collective-permute-start.60 = (bf16[128,2048]{1,0:T(8,128)(2,1)S(1)}, bf16[128,2048]{1,0:T(8,128)(2,1)S(1)}, u32[]{:S(2)}, u32[]{:S(2)}) collective-permute-start(bf16[128,2048]{1,0:T(8,128)(2,1)S(1)} %get-tuple-element.70), channel_id=1, source_target_pairs={{0,1},{1,2},{2,3},{4,5},{5,6},{6,7},{8,9},{9,10},{10,11},{12,13},{... | collective-permute-start | bytes 1572872 | tf_op jit(solution)/shard_map/ppermute | solution.py:39
  790.8 33.2 %collective-permute-start.63 = (bf16[128,2048]{1,0:T(8,128)(2,1)S(1)}, bf16[128,2048]{1,0:T(8,128)(2,1)S(1)}, u32[]{:S(2)}, u32[]{:S(2)}) collective-permute-start(bf16[128,2048]{1,0:T(8,128)(2,1)S(1)} %collective-permute-done.62), channel_id=1, source_target_pairs={{1,0},{5,4},{9,8},{13,12},{17,16},{21,20},{25,24},{29,28}} | collective-permute-start | bytes 1572872 | tf_op jit(solution)/shard_map/ppermute | solution.py:40
  829.3 388.2 %reduce-scatter.17.cloned.1.call-start = ((), (), s32[]{:S(2)}) async-start(), calls=%async_computation.20 | async-start | bytes 2359296 | tf_op jit(solution)/shard_map/reduce_scatter | solution.py:163
  872.6 389.6 %reduce-scatter.9.cloned.1.call-start = ((), (), s32[]{:S(2)}) async-start(), calls=%async_computation.16 | async-start | bytes 5242880 | tf_op jit(solution)/shard_map/reduce_scatter | solution.py:234
  893.2 371.6 %reduce-scatter.23.cloned.1.call-start = ((), (), s32[]{:S(2)}) async-start(), calls=%async_computation.23 | async-start | bytes 2359296 | tf_op jit(solution)/shard_map/reduce_scatter | solution.py:166
  915.2 29.8 %collective-permute-start.67 = (bf16[128,2048]{1,0:T(8,128)(2,1)}, bf16[128,2048]{1,0:T(8,128)(2,1)}, u32[]{:S(2)}, u32[]{:S(2)}) collective-permute-start(bf16[128,2048]{1,0:T(8,128)(2,1)} %get-tuple-element.101), channel_id=1, source_target_pairs={{0,1},{1,2},{4,5},{5,6},{8,9},{9,10},{12,13},{13,14},{16,17},{17,1... | collective-permute-start | bytes 1572872 | tf_op jit(solution)/shard_map/ppermute | solution.py:53
  932.9 46.7 %collective-permute-start.85 = (bf16[128,2048]{1,0:T(8,128)(2,1)}, bf16[128,2048]{1,0:T(8,128)(2,1)}, u32[]{:S(2)}, u32[]{:S(2)}) collective-permute-start(bf16[128,2048]{1,0:T(8,128)(2,1)} %get-tuple-element.113), channel_id=1, source_target_pairs={{0,1},{1,2},{4,5},{5,6},{8,9},{9,10},{12,13},{13,14},{16,17},{17,1... | collective-permute-start | bytes 1572872 | tf_op jit(solution)/shard_map/ppermute | solution.py:53
  943.5 36.1 %collective-permute-start.88 = (bf16[128,2048]{1,0:T(8,128)(2,1)}, bf16[128,2048]{1,0:T(8,128)(2,1)}, u32[]{:S(2)}, u32[]{:S(2)}) collective-permute-start(bf16[128,2048]{1,0:T(8,128)(2,1)} %get-tuple-element.114), channel_id=1, source_target_pairs={{2,1},{3,2},{6,5},{7,6},{10,9},{11,10},{14,13},{15,14},{18,17},{19... | collective-permute-start | bytes 1572872 | tf_op jit(solution)/shard_map/ppermute | solution.py:54
  947.9 46.2 %collective-permute-start.68 = (bf16[128,2048]{1,0:T(8,128)(2,1)}, bf16[128,2048]{1,0:T(8,128)(2,1)}, u32[]{:S(2)}, u32[]{:S(2)}) collective-permute-start(bf16[128,2048]{1,0:T(8,128)(2,1)} %get-tuple-element.99), channel_id=1, source_target_pairs={{0,1},{1,2},{2,3},{4,5},{5,6},{6,7},{8,9},{9,10},{10,11},{12,13},{... | collective-permute-start | bytes 1572872 | tf_op jit(solution)/shard_map/ppermute | solution.py:53
  981.3 31.8 %collective-permute-start.86 = (bf16[128,2048]{1,0:T(8,128)(2,1)S(1)}, bf16[128,2048]{1,0:T(8,128)(2,1)S(1)}, u32[]{:S(2)}, u32[]{:S(2)}) collective-permute-start(bf16[128,2048]{1,0:T(8,128)(2,1)S(1)} %get-tuple-element.111), channel_id=1, source_target_pairs={{0,1},{1,2},{2,3},{4,5},{5,6},{6,7},{8,9},{9,10},{10,11},{12,13},{... | collective-permute-start | bytes 1572872 | tf_op jit(solution)/shard_map/ppermute | solution.py:53
  1018.5 39.3 %collective-permute-start.97 = (bf16[128,2048]{1,0:T(8,128)(2,1)S(1)}, bf16[128,2048]{1,0:T(8,128)(2,1)S(1)}, u32[]{:S(2)}, u32[]{:S(2)}) collective-permute-start(bf16[128,2048]{1,0:T(8,128)(2,1)S(1)} %get-tuple-element.68), channel_id=1, source_target_pairs={{1,0},{2,1},{3,2},{5,4},{6,5},{7,6},{9,8},{10,9},{11,10},{13,12},{... | collective-permute-start | bytes 1572872 | tf_op jit(solution)/shard_map/ppermute | solution.py:40
  1019.9 39.1 %collective-permute-start.96 = (bf16[128,2048]{1,0:T(8,128)(2,1)S(1)}, bf16[128,2048]{1,0:T(8,128)(2,1)S(1)}, u32[]{:S(2)}, u32[]{:S(2)}) collective-permute-start(bf16[128,2048]{1,0:T(8,128)(2,1)S(1)} %get-tuple-element.68), channel_id=1, source_target_pairs={{0,1},{1,2},{2,3},{4,5},{5,6},{6,7},{8,9},{9,10},{10,11},{12,13},{... | collective-permute-start | bytes 1572872 | tf_op jit(solution)/shard_map/ppermute | solution.py:39
  1111.2 189.2 %reduce-scatter.19.cloned.1.call-start = ((), (), s32[]{:S(2)}) async-start(), calls=%async_computation.21 | async-start | bytes 9437184 | tf_op jit(solution)/shard_map/reduce_scatter | solution.py:163
  1111.8 256.9 %reduce-scatter.21.cloned.1.call-start = ((), (), s32[]{:S(2)}) async-start(), calls=%async_computation.22 | async-start | bytes 7077888 | tf_op jit(solution)/shard_map/reduce_scatter | solution.py:163
  1186.6 43.0 %collective-permute-start.108 = (bf16[128,4096]{1,0:T(8,128)(2,1)}, bf16[128,4096]{1,0:T(8,128)(2,1)}, u32[]{:S(2)}, u32[]{:S(2)}) collective-permute-start(bf16[128,4096]{1,0:T(8,128)(2,1)} %dynamic-slice_bitcast_fusion.1), channel_id=1, source_target_pairs={{0,1},{4,5},{8,9},{12,13},{16,17},{20,21},{24,25},{28,29}} | collective-permute-start | bytes 3145736 | tf_op jit(solution)/shard_map/ppermute | solution.py:53
  1208.6 43.4 %collective-permute-start.103 = (bf16[256,2048]{1,0:T(8,128)(2,1)}, bf16[256,2048]{1,0:T(8,128)(2,1)}, u32[]{:S(2)}, u32[]{:S(2)}) collective-permute-start(bf16[256,2048]{1,0:T(8,128)(2,1)} %get-tuple-element.84), channel_id=1, source_target_pairs={{0,1},{1,2},{4,5},{5,6},{8,9},{9,10},{12,13},{13,14},{16,17},{17,1... | collective-permute-start | bytes 3145736 | tf_op jit(solution)/shard_map/ppermute | solution.py:53
  1214.0 38.1 %collective-permute-start.106 = (bf16[256,2048]{1,0:T(8,128)(2,1)S(1)}, bf16[256,2048]{1,0:T(8,128)(2,1)}, u32[]{:S(2)}, u32[]{:S(2)}) collective-permute-start(bf16[256,2048]{1,0:T(8,128)(2,1)S(1)} %get-tuple-element.85), channel_id=1, source_target_pairs={{2,1},{3,2},{6,5},{7,6},{10,9},{11,10},{14,13},{15,14},{18,17},{19... | collective-permute-start | bytes 3145736 | tf_op jit(solution)/shard_map/ppermute | solution.py:54
  1232.3 42.2 %collective-permute-start.109 = (bf16[128,4096]{1,0:T(8,128)(2,1)}, bf16[128,4096]{1,0:T(8,128)(2,1)}, u32[]{:S(2)}, u32[]{:S(2)}) collective-permute-start(bf16[128,4096]{1,0:T(8,128)(2,1)} %fusion.150), channel_id=1, source_target_pairs={{0,1},{1,2},{4,5},{5,6},{8,9},{9,10},{12,13},{13,14},{16,17},{17,1... | collective-permute-start | bytes 3145736 | tf_op jit(solution)/shard_map/ppermute | solution.py:53
  1256.5 40.5 %collective-permute-start.104 = (bf16[256,2048]{1,0:T(8,128)(2,1)}, bf16[256,2048]{1,0:T(8,128)(2,1)S(1)}, u32[]{:S(2)}, u32[]{:S(2)}) collective-permute-start(bf16[256,2048]{1,0:T(8,128)(2,1)} %get-tuple-element.82), channel_id=1, source_target_pairs={{0,1},{1,2},{2,3},{4,5},{5,6},{6,7},{8,9},{9,10},{10,11},{12,13},{... | collective-permute-start | bytes 3145736 | tf_op jit(solution)/shard_map/ppermute | solution.py:53
  1260.9 37.1 %collective-permute-start.107 = (bf16[256,2048]{1,0:T(8,128)(2,1)}, bf16[256,2048]{1,0:T(8,128)(2,1)}, u32[]{:S(2)}, u32[]{:S(2)}) collective-permute-start(bf16[256,2048]{1,0:T(8,128)(2,1)} %get-tuple-element.83), channel_id=1, source_target_pairs={{1,0},{2,1},{3,2},{5,4},{6,5},{7,6},{9,8},{10,9},{11,10},{13,12},{... | collective-permute-start | bytes 3145736 | tf_op jit(solution)/shard_map/ppermute | solution.py:54
  1277.7 87.7 %collective-permute-start.110 = (bf16[128,4096]{1,0:T(8,128)(2,1)}, bf16[128,4096]{1,0:T(8,128)(2,1)}, u32[]{:S(2)}, u32[]{:S(2)}) collective-permute-start(bf16[128,4096]{1,0:T(8,128)(2,1)} %get-tuple-element.64), channel_id=1, source_target_pairs={{0,1},{1,2},{2,3},{4,5},{5,6},{6,7},{8,9},{9,10},{10,11},{12,13},{... | collective-permute-start | bytes 3145736 | tf_op jit(solution)/shard_map/ppermute | solution.py:53
  1318.8 46.6 %collective-permute-start.113 = (bf16[128,4096]{1,0:T(8,128)(2,1)}, bf16[128,4096]{1,0:T(8,128)(2,1)}, u32[]{:S(2)}, u32[]{:S(2)}) collective-permute-start(bf16[128,4096]{1,0:T(8,128)(2,1)} %add_convert_fusion), channel_id=1, source_target_pairs={{1,0},{2,1},{3,2},{5,4},{6,5},{7,6},{9,8},{10,9},{11,10},{13,12},{... | collective-permute-start | bytes 3145736 | tf_op jit(solution)/shard_map/ppermute | solution.py:54
  1321.9 42.8 %collective-permute-start.118 = (f32[3,2,2048]{2,0,1:T(4,128)S(1)}, f32[3,2,2048]{2,0,1:T(4,128)S(1)}, u32[]{:S(2)}, u32[]{:S(2)}) collective-permute-start(f32[3,2,2048]{2,0,1:T(4,128)S(1)} %add.569), channel_id=1, source_target_pairs={{0,2},{1,3},{2,0},{3,1},{4,6},{5,7},{6,4},{7,5},{8,10},{9,11},{10,... | collective-permute-start | bytes 147464 | tf_op jit(solution)/shard_map/ppermute | solution.py:116
  (212 other events, 4728.5 us)
Sparse Core Ops, SparseCore 0:
  11.7 48.1 all-gather.10
  62.3 28.0 all-gather.12
  92.9 27.7 all-gather.18
  122.2 140.3 all-gather.16
  264.8 56.8 all-gather.14
  323.5 28.0 all-gather.20
  353.2 138.1 all-gather.26
  493.9 56.2 all-gather.22
  552.6 55.8 all-gather.24
  659.8 71.4 reduce-scatter.12
  734.8 71.2 reduce-scatter.10
  829.4 46.3 reduce-scatter.14
  879.1 41.1 reduce-scatter.16
  922.4 120.6 reduce-scatter.8
  1111.3 42.6 reduce-scatter.22
  1157.3 71.3 reduce-scatter.18
  1231.9 61.7 reduce-scatter.20
where the time goes:
time: 1390 us; the launch traced here: 1380 us
  waiting for transfers between devices  580 us (42%)
  starting transfers between devices  322 us (23%)
  matrix products  290 us (21%)
  other arithmetic  112 us (8%)
  local copies, waits for them, and re-layouts  48 us (3%)
  between operations  25.5 us (2%)
    ppermute x30, waiting for transfers between devices, sink(): lax.ppermute(one.astype(BF), 'narrow', [(k, k + 1) for k in range(step)])  320 us
    ppermute x27, waiting for transfers between devices, spread(): lax.ppermute(down[-1], 'narrow', [(k, k - 1) for k in range(1, n - step +...  177 us
    ppermute x30, starting transfers between devices, sink(): lax.ppermute(one.astype(BF), 'narrow', [(k, k + 1) for k in range(step)])  142 us
    ppermute x27, starting transfers between devices, spread(): lax.ppermute(up[-1], 'narrow', [(k, k + 1) for k in range(step - 1, n - 1)])  86.5 us
    dot_general x12, matrix products, product(): lax.dot_general(left_side, right_side, (((left_side.ndim - 1,), (0,)), ((...  75.1 us
    dot_general x12, matrix products, right_inner(): lax.dot_general(left_side, right_side, (((left_side.ndim - 1,), (1,)), ((...  69.7 us
    dot_general x7, matrix products, left_inner(): lax.dot_general(left_side, right_side, ((rows, rows), ((), ())), preferre...  57.3 us
    ppermute x27, starting transfers between devices, spread(): lax.ppermute(down[-1], 'narrow', [(k, k - 1) for k in range(1, n - step +...  35.1 us
  transfers between devices with their start and end apart: 136, of which 51 were waited for; matrix products, arithmetic and copies ran while one was open for 29% of the time, Pallas kernels for 0%

commit v1 on v0

--- a/solution.py
+++ b/solution.py
@@ -10,6 +10,18 @@
 MASKED = -1000000000.0
 BF = jnp.bfloat16
 F32 = jnp.float32
+
+
+def gather_by_bits(value, axis, dim):
+    ways, here, hop = (lax.axis_size(axis), lax.axis_index(axis), value.shape[dim])
+    line, have = (value, 1)
+    while have < ways:
+        line = jnp.concatenate(
+            [line, lax.ppermute(line, axis, [(d, (d - have) % ways) for d in range(ways)])],
+            axis=dim,
+        )
+        have = 2 * have
+    return jnp.roll(line, here * hop, axis=dim)
 
 
 def product(left_side, right_side):
@@ -157,7 +169,7 @@
         )
 
     def columns_of(piece):
-        return lax.all_gather(piece.astype(BF), "wide", axis=1, tiled=True)
+        return gather_by_bits(piece.astype(BF), "wide", 1)
 
     def to_rows(g):
         return lax.psum_scatter(g.astype(BF), "wide", scatter_dimension=0, tiled=True).astype(F32)

time: 1390 us -> 1380 us (level)
  waiting for transfers between devices: 580 us -> 513 us
  local copies, waits for them, and re-layouts: 48 us -> 72.6 us
  other arithmetic: 112 us -> 133 us
    ppermute x30, waiting for transfers between devices: 320 us -> 220 us  [sink(): lax.ppermute(one.astype(BF), 'narrow', [(k, k + 1) for k in range(step)])]
    all_gather x1, waiting for transfers between devices: 0.02 us -> 51.5 us  [body(): grad_all = relative(lax.all_gather(out_grad, 'narrow', axis=0))]
    ppermute x0 -> x9, waiting for transfers between devices: none -> 38.2 us  [gather_by_bits(): lax.ppermute(line, axis, [(d, (d - have) % ways) for d in range(ways)])]
    ppermute x27, waiting for transfers between devices: 177 us -> 139 us  [spread(): lax.ppermute(down[-1], 'narrow', [(k, k - 1) for k in range(1, n - step +...]
    all_gather x3 -> x0, waiting for transfers between devices: 32.8 us -> none  [columns_of(): return lax.all_gather(piece.astype(BF), 'wide', axis=1, tiled=True)]
    ppermute x0 -> x9, starting transfers between devices: none -> 32.2 us  [gather_by_bits(): lax.ppermute(line, axis, [(d, (d - have) % ways) for d in range(ways)])]
    ppermute x30, starting transfers between devices: 142 us -> 125 us  [sink(): lax.ppermute(one.astype(BF), 'narrow', [(k, k + 1) for k in range(step)])]
  transfers between devices with their start and end apart: 136 -> 142, of which waited for: 51 -> 57; matrix products, arithmetic and copies ran while one was open for 29% -> 33% of each run, Pallas kernels for 0% -> 0%
where the time goes in v1:
time: 1380 us; the launch traced here: 1370 us
  waiting for transfers between devices  513 us (37%)
  starting transfers between devices  332 us (24%)
  matrix products  288 us (21%)
  other arithmetic  133 us (10%)
  local copies, waits for them, and re-layouts  72.6 us (5%)
  between operations  26.7 us (2%)
    ppermute x30, waiting for transfers between devices, sink(): lax.ppermute(one.astype(BF), 'narrow', [(k, k + 1) for k in range(step)])  220 us
    ppermute x27, waiting for transfers between devices, spread(): lax.ppermute(down[-1], 'narrow', [(k, k - 1) for k in range(1, n - step +...  139 us
    ppermute x30, starting transfers between devices, sink(): lax.ppermute(one.astype(BF), 'narrow', [(k, k + 1) for k in range(step)])  125 us
    ppermute x27, starting transfers between devices, spread(): lax.ppermute(up[-1], 'narrow', [(k, k + 1) for k in range(step - 1, n - 1)])  78.1 us
    dot_general x12, matrix products, product(): lax.dot_general(left_side, right_side, (((left_side.ndim - 1,), (0,)), ((...  76.4 us
    dot_general x12, matrix products, right_inner(): lax.dot_general(left_side, right_side, (((left_side.ndim - 1,), (1,)), ((...  72.1 us
    dot_general x7, matrix products, left_inner(): lax.dot_general(left_side, right_side, ((rows, rows), ((), ())), preferre...  52 us
    all_gather x1, waiting for transfers between devices, body(): grad_all = relative(lax.all_gather(out_grad, 'narrow', axis=0))  51.5 us
  transfers between devices with their start and end apart: 142, of which 57 were waited for; matrix products, arithmetic and copies ran while one was open for 33% of the time, Pallas kernels for 0%

profile of v1, /device:TPU:0, one launch (start us, length us, event | category | flops | bytes accessed | tf_op | source)
XLA Modules:
  0.0 1365.8 jit_solution(9194322029323017892)
XLA Ops:
  43.2 18.0 %collective-permute-done.7 = bf16[512,512]{1,0:T(8,128)(2,1)S(1)} collective-permute-done((bf16[512,512]{1,0:T(8,128)(2,1)}, bf16[512,512]{1,0:T(8,128)(2,1)S(1)}, u32[]{:S(2)}, u32[]{:S(2)}) %collective-permute-start.7) | collective-permute-done | bytes 524320 | tf_op jit(solution)/shard_map/ppermute | solution.py:20
  74.1 20.2 %collective-permute-done.8 = bf16[512,1024]{1,0:T(8,128)(2,1)} collective-permute-done((bf16[512,1024]{1,0:T(8,128)(2,1)}, bf16[512,1024]{1,0:T(8,128)(2,1)}, u32[]{:S(2)}, u32[]{:S(2)}) %collective-permute-start.8) | collective-permute-done | bytes 1048608 | tf_op jit(solution)/shard_map/ppermute | solution.py:20
  103.1 11.8 collective-permute-done.3
  116.0 10.5 fusion.95
  147.0 17.5 %collective-permute-done.9 = bf16[128,2048]{1,0:T(8,128)(2,1)S(1)} collective-permute-done((bf16[128,2048]{1,0:T(8,128)(2,1)S(1)}, bf16[128,2048]{1,0:T(8,128)(2,1)S(1)}, u32[]{:S(2)}, u32[]{:S(2)}) %collective-permute-start.9) | collective-permute-done | bytes 524320 | tf_op jit(solution)/shard_map/ppermute | solution.py:65
  164.5 10.8 collective-permute-start.22
  180.0 7.0 collective-permute-done.30
  194.8 13.1 collective-permute-done.10
  211.2 19.2 %collective-permute-done.31 = bf16[128,2048]{1,0:T(8,128)(2,1)S(1)} collective-permute-done((bf16[128,2048]{1,0:T(8,128)(2,1)S(1)}, bf16[128,2048]{1,0:T(8,128)(2,1)S(1)}, u32[]{:S(2)}, u32[]{:S(2)}) %collective-permute-start.31) | collective-permute-done | bytes 524320 | tf_op jit(solution)/shard_map/ppermute | solution.py:65
  243.7 11.3 collective-permute-start.55
  256.3 16.8 %collective-permute-done.32 = bf16[128,2048]{1,0:T(8,128)(2,1)S(1)} collective-permute-done((bf16[128,2048]{1,0:T(8,128)(2,1)S(1)}, bf16[128,2048]{1,0:T(8,128)(2,1)S(1)}, u32[]{:S(2)}, u32[]{:S(2)}) %collective-permute-start.32) | collective-permute-done | bytes 524320 | tf_op jit(solution)/shard_map/ppermute | solution.py:65
  307.1 7.7 collective-permute-done.17
  317.6 6.5 collective-permute-done.38
  346.3 9.8 all-gather.10.cloned.1.call-done
  356.1 9.1 fusion.232
  397.1 9.9 collective-permute-done.42
  416.2 51.5 %all-gather.18.cloned.1.call-done = bf16[1024,2048]{1,0:T(8,128)(2,1)} async-done(((bf16[256,2048]{1,0:T(8,128)(2,1)}), bf16[1024,2048]{1,0:T(8,128)(2,1)}) %all-gather.18.cloned.1.call-update) | async-done | bytes 4194320 | tf_op jit(solution)/shard_map/all_gather | solution.py:212
  493.1 9.9 collective-permute-start.26
  513.9 8.6 collective-permute-start.48
  554.1 6.6 collective-permute-done.50
  563.5 8.5 collective-permute-done.59
  575.7 7.4 collective-permute-done.51
  584.0 11.9 multiply_convert_fusion.4
  595.9 8.5 fusion.33
  604.4 8.9 fusion.118
  616.2 11.0 multiply_convert_fusion.3
  628.6 11.4 convolution_bitcast_fusion.3
  640.1 10.5 fusion.40
  652.0 11.5 convolution_bitcast_fusion.2
  667.1 8.8 fusion.121
  680.8 8.8 collective-permute-done.81
  724.0 7.1 collective-permute-done.83
  744.4 7.7 collective-permute-done.69
  761.1 6.7 collective-permute-done.88
  770.7 11.8 collective-permute-done.71
  783.8 9.9 collective-permute-done.89
  795.1 15.0 %collective-permute-done.90 = bf16[128,2048]{1,0:T(8,128)(2,1)S(1)} collective-permute-done((bf16[128,2048]{1,0:T(8,128)(2,1)S(1)}, bf16[128,2048]{1,0:T(8,128)(2,1)S(1)}, u32[]{:S(2)}, u32[]{:S(2)}) %collective-permute-start.90) | collective-permute-done | bytes 524320 | tf_op jit(solution)/shard_map/ppermute | solution.py:52
  825.4 9.7 fusion.262
  847.2 9.9 fusion.265
  864.9 8.8 fusion.124
  873.7 8.3 fusion.127
  910.9 9.1 fusion.135
  926.0 12.8 collective-permute-done.76
  949.0 10.2 fusion.236
  964.2 8.4 collective-permute-start.95
  972.6 10.7 collective-permute-done.77
  985.3 14.7 %collective-permute-done.95 = bf16[128,2048]{1,0:T(8,128)(2,1)S(1)} collective-permute-done((bf16[128,2048]{1,0:T(8,128)(2,1)S(1)}, bf16[128,2048]{1,0:T(8,128)(2,1)S(1)}, u32[]{:S(2)}, u32[]{:S(2)}) %collective-permute-start.95) | collective-permute-done | bytes 524320 | tf_op jit(solution)/shard_map/ppermute | solution.py:65
  1005.2 22.6 %collective-permute-start.105 = (bf16[128,2048]{1,0:T(8,128)(2,1)S(1)}, bf16[128,2048]{1,0:T(8,128)(2,1)S(1)}, u32[]{:S(2)}, u32[]{:S(2)}) collective-permute-start(bf16[128,2048]{1,0:T(8,128)(2,1)S(1)} %get-tuple-element.69), channel_id=1, source_target_pairs={{0,1},{1,2},{2,3},{4,5},{5,6},{6,7},{8,9},{9,10},{10,11},{12,13},{... | collective-permute-start | bytes 1572872 | tf_op jit(solution)/shard_map/ppermute | solution.py:51
  1035.1 6.7 convolution_bitcast_fusion.1
  1047.8 8.0 collective-permute-done.100
  1057.3 10.2 convolution_convert_fusion
  1070.3 8.0 collective-permute-done.101
  1079.7 9.8 collective-permute-done.108
  1125.4 9.8 fusion.229
  1136.7 9.7 fusion.226
  1151.3 8.8 convolution_bitcast_fusion
  1160.1 10.1 fusion.98
  1177.5 18.1 %collective-permute-done.111 = bf16[256,2048]{1,0:T(8,128)(2,1)S(1)} collective-permute-done((bf16[256,2048]{1,0:T(8,128)(2,1)S(1)}, bf16[256,2048]{1,0:T(8,128)(2,1)S(1)}, u32[]{:S(2)}, u32[]{:S(2)}) %collective-permute-start.111) | collective-permute-done | bytes 1048608 | tf_op jit(solution)/shard_map/ppermute | solution.py:65
  1208.0 10.2 collective-permute-done.117
  1226.3 14.4 %collective-permute-done.112 = bf16[256,2048]{1,0:T(8,128)(2,1)} collective-permute-done((bf16[256,2048]{1,0:T(8,128)(2,1)}, bf16[256,2048]{1,0:T(8,128)(2,1)}, u32[]{:S(2)}, u32[]{:S(2)}) %collective-permute-start.112) | collective-permute-done | bytes 1048608 | tf_op jit(solution)/shard_map/ppermute | solution.py:65
  1246.7 6.6 collective-permute-start.113
  1274.4 11.3 collective-permute-done.113
  1309.7 19.2 %collective-permute-start.127 = (f32[3,2,2048]{2,0,1:T(4,128)S(1)}, f32[3,2,2048]{2,0,1:T(4,128)S(1)}, u32[]{:S(2)}, u32[]{:S(2)}) collective-permute-start(f32[3,2,2048]{2,0,1:T(4,128)S(1)} %add.588), channel_id=1, source_target_pairs={{0,2},{1,3},{2,0},{3,1},{4,6},{5,7},{6,4},{7,5},{8,10},{9,11},{10,... | collective-permute-start | bytes 147464 | tf_op jit(solution)/shard_map/ppermute | solution.py:128
  1331.8 20.7 %collective-permute-done.127 = f32[3,2,2048]{2,0,1:T(4,128)S(1)} collective-permute-done((f32[3,2,2048]{2,0,1:T(4,128)S(1)}, f32[3,2,2048]{2,0,1:T(4,128)S(1)}, u32[]{:S(2)}, u32[]{:S(2)}) %collective-permute-start.127) | collective-permute-done | bytes 49184 | tf_op jit(solution)/shard_map/ppermute | solution.py:128
  (824 shorter events, 591.0 us)
Async XLA Ops:
  7.2 108.7 %all-gather.8.cloned.1.call-start = ((), (), s32[]{:S(2)}) async-start(), calls=%async_computation.8 | async-start | bytes 7077888 | tf_op jit(solution)/shard_map/all_gather | solution.py:167
  11.6 318.9 %all-gather.14.cloned.1.call-start = ((), (), s32[]{:S(2)}) async-start(), calls=%async_computation.11 | async-start | bytes 2359296 | tf_op jit(solution)/shard_map/all_gather | solution.py:167
  13.5 332.8 %all-gather.12.cloned.1.call-start = ((), (), s32[]{:S(2)}) async-start(), calls=%async_computation.10 | async-start | bytes 5242880 | tf_op jit(solution)/shard_map/all_gather | solution.py:198
  14.2 341.9 %all-gather.10.cloned.1.call-start = ((), (), s32[]{:S(2)}) async-start(), calls=%async_computation.9 | async-start | bytes 9437184 | tf_op jit(solution)/shard_map/all_gather | solution.py:167
  15.7 452.1 %all-gather.18.cloned.1.call-start = ((), (), s32[]{:S(2)}) async-start(), calls=%async_computation.21 | async-start | bytes 5242880 | tf_op jit(solution)/shard_map/all_gather | solution.py:212
  16.3 567.7 %all-gather.16.cloned.1.call-start = ((), (), s32[]{:S(2)}) async-start(), calls=%async_computation.12 | async-start | bytes 9437184 | tf_op jit(solution)/shard_map/all_gather | solution.py:167
  18.5 45.3 %collective-permute-start = (bf16[256,2048]{1,0:T(8,128)(2,1)}, bf16[256,2048]{1,0:T(8,128)(2,1)}, u32[]{:S(2)}, u32[]{:S(2)}) collective-permute-start(bf16[256,2048]{1,0:T(8,128)(2,1)} %add_convert_fusion.4), channel_id=1, source_target_pairs={{0,1},{1,2},{2,3},{4,5},{5,6},{6,7},{8,9},{9,10},{10,11},{12,13},{... | collective-permute-start | bytes 3145736 | tf_op jit(solution)/shard_map/ppermute | solution.py:51
  24.5 46.1 %collective-permute-start.1 = (bf16[256,2048]{1,0:T(8,128)(2,1)}, bf16[256,2048]{1,0:T(8,128)(2,1)}, u32[]{:S(2)}, u32[]{:S(2)}) collective-permute-start(bf16[256,2048]{1,0:T(8,128)(2,1)} %add_convert_fusion.4), channel_id=1, source_target_pairs={{1,0},{2,1},{3,2},{5,4},{6,5},{7,6},{9,8},{10,9},{11,10},{13,12},{... | collective-permute-start | bytes 3145736 | tf_op jit(solution)/shard_map/ppermute | solution.py:52
  27.5 117.8 %collective-permute-start.21 = (bf16[512,256]{1,0:T(8,128)(2,1)S(1)}, bf16[512,256]{1,0:T(8,128)(2,1)}, u32[]{:S(2)}, u32[]{:S(2)}) collective-permute-start(bf16[512,256]{1,0:T(8,128)(2,1)S(1)} %convert_element_type.822), channel_id=1, source_target_pairs={{0,28},{4,0},{8,4},{12,8},{16,12},{20,16},{24,20},{28,24},{1,29},{... | collective-permute-start | bytes 786440 | tf_op jit(solution)/shard_map/ppermute | solution.py:20
  31.6 205.1 %collective-permute-start.54 = (bf16[2048,256]{1,0:T(8,128)(2,1)}, bf16[2048,256]{1,0:T(8,128)(2,1)S(1)}, u32[]{:S(2)}, u32[]{:S(2)}) collective-permute-start(bf16[2048,256]{1,0:T(8,128)(2,1)} %get-tuple-element.78), channel_id=1, source_target_pairs={{0,28},{4,0},{8,4},{12,8},{16,12},{20,16},{24,20},{28,24},{1,29},{... | collective-permute-start | bytes 3145736 | tf_op jit(solution)/shard_map/ppermute | solution.py:20
  32.7 1076.0 %reduce-scatter.11.cloned.1.call-start = ((), (), s32[]{:S(2)}) async-start(), calls=%async_computation.14 | async-start | bytes 9437184 | tf_op jit(solution)/shard_map/reduce_scatter | solution.py:178
  35.2 26.0 %collective-permute-start.7 = (bf16[512,512]{1,0:T(8,128)(2,1)}, bf16[512,512]{1,0:T(8,128)(2,1)S(1)}, u32[]{:S(2)}, u32[]{:S(2)}) collective-permute-start(bf16[512,512]{1,0:T(8,128)(2,1)} %pad_maximum_fusion.18), channel_id=1, source_target_pairs={{0,24},{4,28},{8,0},{12,4},{16,8},{20,12},{24,16},{28,20},{1,25},{... | collective-permute-start | bytes 1572872 | tf_op jit(solution)/shard_map/ppermute | solution.py:20
  62.4 31.8 %collective-permute-start.8 = (bf16[512,1024]{1,0:T(8,128)(2,1)}, bf16[512,1024]{1,0:T(8,128)(2,1)}, u32[]{:S(2)}, u32[]{:S(2)}) collective-permute-start(bf16[512,1024]{1,0:T(8,128)(2,1)} %pad_maximum_fusion.8), channel_id=1, source_target_pairs={{0,16},{4,20},{8,24},{12,28},{16,0},{20,4},{24,8},{28,12},{1,17},{... | collective-permute-start | bytes 3145736 | tf_op jit(solution)/shard_map/ppermute | solution.py:20
  70.6 27.6 %collective-permute-start.2 = (bf16[256,2048]{1,0:T(8,128)(2,1)}, bf16[256,2048]{1,0:T(8,128)(2,1)S(1)}, u32[]{:S(2)}, u32[]{:S(2)}) collective-permute-start(bf16[256,2048]{1,0:T(8,128)(2,1)} %collective-permute-done.1), channel_id=1, source_target_pairs={{1,0},{2,1},{5,4},{6,5},{9,8},{10,9},{13,12},{14,13},{17,16},{18,1... | collective-permute-start | bytes 3145736 | tf_op jit(solution)/shard_map/ppermute | solution.py:52
  73.3 27.5 %collective-permute-start.5 = (bf16[256,2048]{1,0:T(8,128)(2,1)}, bf16[256,2048]{1,0:T(8,128)(2,1)S(1)}, u32[]{:S(2)}, u32[]{:S(2)}) collective-permute-start(bf16[256,2048]{1,0:T(8,128)(2,1)} %collective-permute-done.4), channel_id=1, source_target_pairs={{2,3},{6,7},{10,11},{14,15},{18,19},{22,23},{26,27},{30,31}} | collective-permute-start | bytes 3145736 | tf_op jit(solution)/shard_map/ppermute | solution.py:51
  143.2 32.2 %collective-permute-start.12 = (bf16[128,2048]{1,0:T(8,128)(2,1)S(1)}, bf16[128,2048]{1,0:T(8,128)(2,1)S(1)}, u32[]{:S(2)}, u32[]{:S(2)}) collective-permute-start(bf16[128,2048]{1,0:T(8,128)(2,1)S(1)} %get-tuple-element.145), channel_id=1, source_target_pairs={{3,2},{7,6},{11,10},{15,14},{19,18},{23,22},{27,26},{31,30}} | collective-permute-start | bytes 1572872 | tf_op jit(solution)/shard_map/ppermute | solution.py:66
  144.0 43.0 %collective-permute-start.30 = (bf16[128,2048]{1,0:T(8,128)(2,1)S(1)}, bf16[128,2048]{1,0:T(8,128)(2,1)S(1)}, u32[]{:S(2)}, u32[]{:S(2)}) collective-permute-start(bf16[128,2048]{1,0:T(8,128)(2,1)S(1)} %get-tuple-element.150), channel_id=1, source_target_pairs={{0,1},{4,5},{8,9},{12,13},{16,17},{20,21},{24,25},{28,29}} | collective-permute-start | bytes 1572872 | tf_op jit(solution)/shard_map/ppermute | solution.py:65
  145.3 42.4 %collective-permute-start.33 = (bf16[128,2048]{1,0:T(8,128)(2,1)S(1)}, bf16[128,2048]{1,0:T(8,128)(2,1)S(1)}, u32[]{:S(2)}, u32[]{:S(2)}) collective-permute-start(bf16[128,2048]{1,0:T(8,128)(2,1)S(1)} %get-tuple-element.151), channel_id=1, source_target_pairs={{3,2},{7,6},{11,10},{15,14},{19,18},{23,22},{27,26},{31,30}} | collective-permute-start | bytes 1572872 | tf_op jit(solution)/shard_map/ppermute | solution.py:66
  164.5 28.5 %collective-permute-start.22 = (bf16[512,512]{1,0:T(8,128)(2,1)S(1)}, bf16[512,512]{1,0:T(8,128)(2,1)S(1)}, u32[]{:S(2)}, u32[]{:S(2)}) collective-permute-start(bf16[512,512]{1,0:T(8,128)(2,1)S(1)} %pad_maximum_fusion.19), channel_id=1, source_target_pairs={{0,24},{4,28},{8,0},{12,4},{16,8},{20,12},{24,16},{28,20},{1,25},{... | collective-permute-start | bytes 1572872 | tf_op jit(solution)/shard_map/ppermute | solution.py:20
  175.6 32.3 %collective-permute-start.10 = (bf16[128,2048]{1,0:T(8,128)(2,1)S(1)}, bf16[128,2048]{1,0:T(8,128)(2,1)S(1)}, u32[]{:S(2)}, u32[]{:S(2)}) collective-permute-start(bf16[128,2048]{1,0:T(8,128)(2,1)S(1)} %get-tuple-element.142), channel_id=1, source_target_pairs={{0,1},{1,2},{4,5},{5,6},{8,9},{9,10},{12,13},{13,14},{16,17},{17,1... | collective-permute-start | bytes 1572872 | tf_op jit(solution)/shard_map/ppermute | solution.py:65
  188.0 42.4 %collective-permute-start.31 = (bf16[128,2048]{1,0:T(8,128)(2,1)S(1)}, bf16[128,2048]{1,0:T(8,128)(2,1)S(1)}, u32[]{:S(2)}, u32[]{:S(2)}) collective-permute-start(bf16[128,2048]{1,0:T(8,128)(2,1)S(1)} %get-tuple-element.148), channel_id=1, source_target_pairs={{0,1},{1,2},{4,5},{5,6},{8,9},{9,10},{12,13},{13,14},{16,17},{17,1... | collective-permute-start | bytes 1572872 | tf_op jit(solution)/shard_map/ppermute | solution.py:65
  193.0 41.9 %collective-permute-start.34 = (bf16[128,2048]{1,0:T(8,128)(2,1)S(1)}, bf16[128,2048]{1,0:T(8,128)(2,1)S(1)}, u32[]{:S(2)}, u32[]{:S(2)}) collective-permute-start(bf16[128,2048]{1,0:T(8,128)(2,1)S(1)} %get-tuple-element.149), channel_id=1, source_target_pairs={{2,1},{3,2},{6,5},{7,6},{10,9},{11,10},{14,13},{15,14},{18,17},{19... | collective-permute-start | bytes 1572872 | tf_op jit(solution)/shard_map/ppermute | solution.py:66
  207.9 77.3 %collective-permute-start.23 = (bf16[512,1024]{1,0:T(8,128)(2,1)S(1)}, bf16[512,1024]{1,0:T(8,128)(2,1)S(1)}, u32[]{:S(2)}, u32[]{:S(2)}) collective-permute-start(bf16[512,1024]{1,0:T(8,128)(2,1)S(1)} %pad_maximum_fusion.10), channel_id=1, source_target_pairs={{0,16},{4,20},{8,24},{12,28},{16,0},{20,4},{24,8},{28,12},{1,17},{... | collective-permute-start | bytes 3145736 | tf_op jit(solution)/shard_map/ppermute | solution.py:20
  209.9 33.9 %collective-permute-start.14 = (bf16[128,2048]{1,0:T(8,128)(2,1)S(1)}, bf16[128,2048]{1,0:T(8,128)(2,1)S(1)}, u32[]{:S(2)}, u32[]{:S(2)}) collective-permute-start(bf16[128,2048]{1,0:T(8,128)(2,1)S(1)} %get-tuple-element.141), channel_id=1, source_target_pairs={{1,0},{2,1},{3,2},{5,4},{6,5},{7,6},{9,8},{10,9},{11,10},{13,12},{... | collective-permute-start | bytes 1572872 | tf_op jit(solution)/shard_map/ppermute | solution.py:66
  230.4 25.9 %collective-permute-start.11 = (bf16[128,2048]{1,0:T(8,128)(2,1)S(1)}, bf16[128,2048]{1,0:T(8,128)(2,1)S(1)}, u32[]{:S(2)}, u32[]{:S(2)}) collective-permute-start(bf16[128,2048]{1,0:T(8,128)(2,1)S(1)} %get-tuple-element.140), channel_id=1, source_target_pairs={{0,1},{1,2},{2,3},{4,5},{5,6},{6,7},{8,9},{9,10},{10,11},{12,13},{... | collective-permute-start | bytes 1572872 | tf_op jit(solution)/shard_map/ppermute | solution.py:65
  236.7 36.5 %collective-permute-start.32 = (bf16[128,2048]{1,0:T(8,128)(2,1)S(1)}, bf16[128,2048]{1,0:T(8,128)(2,1)S(1)}, u32[]{:S(2)}, u32[]{:S(2)}) collective-permute-start(bf16[128,2048]{1,0:T(8,128)(2,1)S(1)} %get-tuple-element.146), channel_id=1, source_target_pairs={{0,1},{1,2},{2,3},{4,5},{5,6},{6,7},{8,9},{9,10},{10,11},{12,13},{... | collective-permute-start | bytes 1572872 | tf_op jit(solution)/shard_map/ppermute | solution.py:65
  243.7 49.9 %collective-permute-start.55 = (bf16[2048,512]{1,0:T(8,128)(2,1)S(1)}, bf16[2048,512]{1,0:T(8,128)(2,1)S(1)}, u32[]{:S(2)}, u32[]{:S(2)}) collective-permute-start(bf16[2048,512]{1,0:T(8,128)(2,1)S(1)} %pad_maximum_fusion.5), channel_id=1, source_target_pairs={{0,24},{4,28},{8,0},{12,4},{16,8},{20,12},{24,16},{28,20},{1,25},{... | collective-permute-start | bytes 6291464 | tf_op jit(solution)/shard_map/ppermute | solution.py:20
  297.3 226.6 %collective-permute-start.56 = (bf16[2048,1024]{1,0:T(8,128)(2,1)}, bf16[2048,1024]{1,0:T(8,128)(2,1)}, u32[]{:S(2)}, u32[]{:S(2)}) collective-permute-start(bf16[2048,1024]{1,0:T(8,128)(2,1)} %pad_maximum_fusion.1), channel_id=1, source_target_pairs={{0,16},{4,20},{8,24},{12,28},{16,0},{20,4},{24,8},{28,12},{1,17},{... | collective-permute-start | bytes 12582920 | tf_op jit(solution)/shard_map/ppermute | solution.py:20
  379.6 27.3 %collective-permute-start.42 = (bf16[128,2048]{1,0:T(8,128)(2,1)}, bf16[128,2048]{1,0:T(8,128)(2,1)}, u32[]{:S(2)}, u32[]{:S(2)}) collective-permute-start(bf16[128,2048]{1,0:T(8,128)(2,1)} %get-tuple-element.136), channel_id=1, source_target_pairs={{0,1},{4,5},{8,9},{12,13},{16,17},{20,21},{24,25},{28,29}} | collective-permute-start | bytes 1572872 | tf_op jit(solution)/shard_map/ppermute | solution.py:65
  394.2 76.5 %collective-permute-start.24 = (bf16[128,2048]{1,0:T(8,128)(2,1)}, bf16[128,2048]{1,0:T(8,128)(2,1)S(1)}, u32[]{:S(2)}, u32[]{:S(2)}) collective-permute-start(bf16[128,2048]{1,0:T(8,128)(2,1)} %get-tuple-element.130), channel_id=1, source_target_pairs={{0,1},{4,5},{8,9},{12,13},{16,17},{20,21},{24,25},{28,29}} | collective-permute-start | bytes 1572872 | tf_op jit(solution)/shard_map/ppermute | solution.py:65
  395.5 75.2 %collective-permute-start.27 = (bf16[128,2048]{1,0:T(8,128)(2,1)}, bf16[128,2048]{1,0:T(8,128)(2,1)}, u32[]{:S(2)}, u32[]{:S(2)}) collective-permute-start(bf16[128,2048]{1,0:T(8,128)(2,1)} %get-tuple-element.131), channel_id=1, source_target_pairs={{3,2},{7,6},{11,10},{15,14},{19,18},{23,22},{27,26},{31,30}} | collective-permute-start | bytes 1572872 | tf_op jit(solution)/shard_map/ppermute | solution.py:66
  409.6 70.2 %collective-permute-start.43 = (bf16[128,2048]{1,0:T(8,128)(2,1)}, bf16[128,2048]{1,0:T(8,128)(2,1)}, u32[]{:S(2)}, u32[]{:S(2)}) collective-permute-start(bf16[128,2048]{1,0:T(8,128)(2,1)} %get-tuple-element.134), channel_id=1, source_target_pairs={{0,1},{1,2},{4,5},{5,6},{8,9},{9,10},{12,13},{13,14},{16,17},{17,1... | collective-permute-start | bytes 1572872 | tf_op jit(solution)/shard_map/ppermute | solution.py:65
  414.8 65.1 %collective-permute-start.46 = (bf16[128,2048]{1,0:T(8,128)(2,1)}, bf16[128,2048]{1,0:T(8,128)(2,1)}, u32[]{:S(2)}, u32[]{:S(2)}) collective-permute-start(bf16[128,2048]{1,0:T(8,128)(2,1)} %get-tuple-element.135), channel_id=1, source_target_pairs={{2,1},{3,2},{6,5},{7,6},{10,9},{11,10},{14,13},{15,14},{18,17},{19... | collective-permute-start | bytes 1572872 | tf_op jit(solution)/shard_map/ppermute | solution.py:66
  562.0 52.6 %collective-permute-start.62 = (bf16[128,2048]{1,0:T(8,128)(2,1)}, bf16[128,2048]{1,0:T(8,128)(2,1)}, u32[]{:S(2)}, u32[]{:S(2)}) collective-permute-start(bf16[128,2048]{1,0:T(8,128)(2,1)} %collective-permute-done.61), channel_id=1, source_target_pairs={{2,3},{6,7},{10,11},{14,15},{18,19},{22,23},{26,27},{30,31}} | collective-permute-start | bytes 1572872 | tf_op jit(solution)/shard_map/ppermute | solution.py:51
  573.1 41.6 %collective-permute-start.60 = (bf16[128,2048]{1,0:T(8,128)(2,1)}, bf16[128,2048]{1,0:T(8,128)(2,1)}, u32[]{:S(2)}, u32[]{:S(2)}) collective-permute-start(bf16[128,2048]{1,0:T(8,128)(2,1)} %collective-permute-done.59), channel_id=1, source_target_pairs={{1,0},{5,4},{9,8},{13,12},{17,16},{21,20},{25,24},{29,28}} | collective-permute-start | bytes 1572872 | tf_op jit(solution)/shard_map/ppermute | solution.py:52
  640.0 471.5 %reduce-scatter.13.cloned.1.call-start = ((), (), s32[]{:S(2)}) async-start(), calls=%async_computation.15 | async-start | bytes 9437184 | tf_op jit(solution)/shard_map/reduce_scatter | solution.py:175
  663.5 540.8 %reduce-scatter.15.cloned.1.call-start = ((), (), s32[]{:S(2)}) async-start(), calls=%async_computation.16 | async-start | bytes 2359296 | tf_op jit(solution)/shard_map/reduce_scatter | solution.py:178
  767.8 25.9 %collective-permute-start.89 = (bf16[128,2048]{1,0:T(8,128)(2,1)S(1)}, bf16[128,2048]{1,0:T(8,128)(2,1)S(1)}, u32[]{:S(2)}, u32[]{:S(2)}) collective-permute-start(bf16[128,2048]{1,0:T(8,128)(2,1)S(1)} %collective-permute-done.88), channel_id=1, source_target_pairs={{1,0},{2,1},{5,4},{6,5},{9,8},{10,9},{13,12},{14,13},{17,16},{18,1... | collective-permute-start | bytes 1572872 | tf_op jit(solution)/shard_map/ppermute | solution.py:52
  769.3 41.2 %collective-permute-start.74 = (bf16[128,2048]{1,0:T(8,128)(2,1)S(1)}, bf16[128,2048]{1,0:T(8,128)(2,1)S(1)}, u32[]{:S(2)}, u32[]{:S(2)}) collective-permute-start(bf16[128,2048]{1,0:T(8,128)(2,1)S(1)} %collective-permute-done.73), channel_id=1, source_target_pairs={{2,3},{6,7},{10,11},{14,15},{18,19},{22,23},{26,27},{30,31}} | collective-permute-start | bytes 1572872 | tf_op jit(solution)/shard_map/ppermute | solution.py:51
  782.5 28.0 %collective-permute-start.72 = (bf16[128,2048]{1,0:T(8,128)(2,1)S(1)}, bf16[128,2048]{1,0:T(8,128)(2,1)S(1)}, u32[]{:S(2)}, u32[]{:S(2)}) collective-permute-start(bf16[128,2048]{1,0:T(8,128)(2,1)S(1)} %collective-permute-done.71), channel_id=1, source_target_pairs={{1,0},{5,4},{9,8},{13,12},{17,16},{21,20},{25,24},{29,28}} | collective-permute-start | bytes 1572872 | tf_op jit(solution)/shard_map/ppermute | solution.py:52
  815.6 390.6 %reduce-scatter.17.cloned.1.call-start = ((), (), s32[]{:S(2)}) async-start(), calls=%async_computation.17 | async-start | bytes 2359296 | tf_op jit(solution)/shard_map/reduce_scatter | solution.py:175
  864.6 388.7 %reduce-scatter.9.cloned.1.call-start = ((), (), s32[]{:S(2)}) async-start(), calls=%async_computation.13 | async-start | bytes 5242880 | tf_op jit(solution)/shard_map/reduce_scatter | solution.py:246
  885.0 370.8 %reduce-scatter.23.cloned.1.call-start = ((), (), s32[]{:S(2)}) async-start(), calls=%async_computation.20 | async-start | bytes 2359296 | tf_op jit(solution)/shard_map/reduce_scatter | solution.py:178
  903.9 34.9 %collective-permute-start.76 = (bf16[128,2048]{1,0:T(8,128)(2,1)}, bf16[128,2048]{1,0:T(8,128)(2,1)}, u32[]{:S(2)}, u32[]{:S(2)}) collective-permute-start(bf16[128,2048]{1,0:T(8,128)(2,1)} %get-tuple-element.104), channel_id=1, source_target_pairs={{0,1},{1,2},{4,5},{5,6},{8,9},{9,10},{12,13},{13,14},{16,17},{17,1... | collective-permute-start | bytes 1572872 | tf_op jit(solution)/shard_map/ppermute | solution.py:65
  909.1 29.7 %collective-permute-start.79 = (bf16[128,2048]{1,0:T(8,128)(2,1)S(1)}, bf16[128,2048]{1,0:T(8,128)(2,1)}, u32[]{:S(2)}, u32[]{:S(2)}) collective-permute-start(bf16[128,2048]{1,0:T(8,128)(2,1)S(1)} %get-tuple-element.105), channel_id=1, source_target_pairs={{2,1},{3,2},{6,5},{7,6},{10,9},{11,10},{14,13},{15,14},{18,17},{19... | collective-permute-start | bytes 1572872 | tf_op jit(solution)/shard_map/ppermute | solution.py:66
  922.5 38.8 %collective-permute-start.94 = (bf16[128,2048]{1,0:T(8,128)(2,1)}, bf16[128,2048]{1,0:T(8,128)(2,1)}, u32[]{:S(2)}, u32[]{:S(2)}) collective-permute-start(bf16[128,2048]{1,0:T(8,128)(2,1)} %get-tuple-element.116), channel_id=1, source_target_pairs={{0,1},{1,2},{4,5},{5,6},{8,9},{9,10},{12,13},{13,14},{16,17},{17,1... | collective-permute-start | bytes 1572872 | tf_op jit(solution)/shard_map/ppermute | solution.py:65
  924.6 36.7 %collective-permute-start.97 = (bf16[128,2048]{1,0:T(8,128)(2,1)}, bf16[128,2048]{1,0:T(8,128)(2,1)}, u32[]{:S(2)}, u32[]{:S(2)}) collective-permute-start(bf16[128,2048]{1,0:T(8,128)(2,1)} %get-tuple-element.117), channel_id=1, source_target_pairs={{2,1},{3,2},{6,5},{7,6},{10,9},{11,10},{14,13},{15,14},{18,17},{19... | collective-permute-start | bytes 1572872 | tf_op jit(solution)/shard_map/ppermute | solution.py:66
  941.7 30.9 %collective-permute-start.80 = (bf16[128,2048]{1,0:T(8,128)(2,1)}, bf16[128,2048]{1,0:T(8,128)(2,1)}, u32[]{:S(2)}, u32[]{:S(2)}) collective-permute-start(bf16[128,2048]{1,0:T(8,128)(2,1)} %get-tuple-element.103), channel_id=1, source_target_pairs={{1,0},{2,1},{3,2},{5,4},{6,5},{7,6},{9,8},{10,9},{11,10},{13,12},{... | collective-permute-start | bytes 1572872 | tf_op jit(solution)/shard_map/ppermute | solution.py:66
  943.0 40.3 %collective-permute-start.77 = (bf16[128,2048]{1,0:T(8,128)(2,1)}, bf16[128,2048]{1,0:T(8,128)(2,1)}, u32[]{:S(2)}, u32[]{:S(2)}) collective-permute-start(bf16[128,2048]{1,0:T(8,128)(2,1)} %get-tuple-element.102), channel_id=1, source_target_pairs={{0,1},{1,2},{2,3},{4,5},{5,6},{6,7},{8,9},{9,10},{10,11},{12,13},{... | collective-permute-start | bytes 1572872 | tf_op jit(solution)/shard_map/ppermute | solution.py:65
  964.2 35.8 %collective-permute-start.95 = (bf16[128,2048]{1,0:T(8,128)(2,1)S(1)}, bf16[128,2048]{1,0:T(8,128)(2,1)S(1)}, u32[]{:S(2)}, u32[]{:S(2)}) collective-permute-start(bf16[128,2048]{1,0:T(8,128)(2,1)S(1)} %get-tuple-element.114), channel_id=1, source_target_pairs={{0,1},{1,2},{2,3},{4,5},{5,6},{6,7},{8,9},{9,10},{10,11},{12,13},{... | collective-permute-start | bytes 1572872 | tf_op jit(solution)/shard_map/ppermute | solution.py:65
  1005.2 36.5 %collective-permute-start.105 = (bf16[128,2048]{1,0:T(8,128)(2,1)S(1)}, bf16[128,2048]{1,0:T(8,128)(2,1)S(1)}, u32[]{:S(2)}, u32[]{:S(2)}) collective-permute-start(bf16[128,2048]{1,0:T(8,128)(2,1)S(1)} %get-tuple-element.69), channel_id=1, source_target_pairs={{0,1},{1,2},{2,3},{4,5},{5,6},{6,7},{8,9},{9,10},{10,11},{12,13},{... | collective-permute-start | bytes 1572872 | tf_op jit(solution)/shard_map/ppermute | solution.py:51
  1041.8 25.7 %collective-permute-start.109 = (bf16[128,2048]{1,0:T(8,128)(2,1)S(1)}, bf16[128,2048]{1,0:T(8,128)(2,1)S(1)}, u32[]{:S(2)}, u32[]{:S(2)}) collective-permute-start(bf16[128,2048]{1,0:T(8,128)(2,1)S(1)} %collective-permute-done.105), channel_id=1, source_target_pairs={{1,2},{2,3},{5,6},{6,7},{9,10},{10,11},{13,14},{14,15},{17,18},{18... | collective-permute-start | bytes 1572872 | tf_op jit(solution)/shard_map/ppermute | solution.py:51
  1101.2 186.9 %reduce-scatter.19.cloned.1.call-start = ((), (), s32[]{:S(2)}) async-start(), calls=%async_computation.18 | async-start | bytes 9437184 | tf_op jit(solution)/shard_map/reduce_scatter | solution.py:175
  1101.9 254.5 %reduce-scatter.21.cloned.1.call-start = ((), (), s32[]{:S(2)}) async-start(), calls=%async_computation.19 | async-start | bytes 7077888 | tf_op jit(solution)/shard_map/reduce_scatter | solution.py:175
  1170.5 25.1 %collective-permute-start.111 = (bf16[256,2048]{1,0:T(8,128)(2,1)S(1)}, bf16[256,2048]{1,0:T(8,128)(2,1)S(1)}, u32[]{:S(2)}, u32[]{:S(2)}) collective-permute-start(bf16[256,2048]{1,0:T(8,128)(2,1)S(1)} %get-tuple-element.89), channel_id=1, source_target_pairs={{0,1},{4,5},{8,9},{12,13},{16,17},{20,21},{24,25},{28,29}} | collective-permute-start | bytes 3145736 | tf_op jit(solution)/shard_map/ppermute | solution.py:65
  1175.2 43.0 %collective-permute-start.117 = (bf16[128,4096]{1,0:T(8,128)(2,1)}, bf16[128,4096]{1,0:T(8,128)(2,1)}, u32[]{:S(2)}, u32[]{:S(2)}) collective-permute-start(bf16[128,4096]{1,0:T(8,128)(2,1)} %dynamic-slice_bitcast_fusion.1), channel_id=1, source_target_pairs={{0,1},{4,5},{8,9},{12,13},{16,17},{20,21},{24,25},{28,29}} | collective-permute-start | bytes 3145736 | tf_op jit(solution)/shard_map/ppermute | solution.py:65
  1197.3 43.4 %collective-permute-start.112 = (bf16[256,2048]{1,0:T(8,128)(2,1)}, bf16[256,2048]{1,0:T(8,128)(2,1)}, u32[]{:S(2)}, u32[]{:S(2)}) collective-permute-start(bf16[256,2048]{1,0:T(8,128)(2,1)} %get-tuple-element.87), channel_id=1, source_target_pairs={{0,1},{1,2},{4,5},{5,6},{8,9},{9,10},{12,13},{13,14},{16,17},{17,1... | collective-permute-start | bytes 3145736 | tf_op jit(solution)/shard_map/ppermute | solution.py:65
  1202.7 38.0 %collective-permute-start.115 = (bf16[256,2048]{1,0:T(8,128)(2,1)S(1)}, bf16[256,2048]{1,0:T(8,128)(2,1)}, u32[]{:S(2)}, u32[]{:S(2)}) collective-permute-start(bf16[256,2048]{1,0:T(8,128)(2,1)S(1)} %get-tuple-element.88), channel_id=1, source_target_pairs={{2,1},{3,2},{6,5},{7,6},{10,9},{11,10},{14,13},{15,14},{18,17},{19... | collective-permute-start | bytes 3145736 | tf_op jit(solution)/shard_map/ppermute | solution.py:66
  1221.0 42.2 %collective-permute-start.118 = (bf16[128,4096]{1,0:T(8,128)(2,1)}, bf16[128,4096]{1,0:T(8,128)(2,1)}, u32[]{:S(2)}, u32[]{:S(2)}) collective-permute-start(bf16[128,4096]{1,0:T(8,128)(2,1)} %fusion.154), channel_id=1, source_target_pairs={{0,1},{1,2},{4,5},{5,6},{8,9},{9,10},{12,13},{13,14},{16,17},{17,1... | collective-permute-start | bytes 3145736 | tf_op jit(solution)/shard_map/ppermute | solution.py:65
  1245.4 28.0 %collective-permute-start.116 = (bf16[256,2048]{1,0:T(8,128)(2,1)}, bf16[256,2048]{1,0:T(8,128)(2,1)S(1)}, u32[]{:S(2)}, u32[]{:S(2)}) collective-permute-start(bf16[256,2048]{1,0:T(8,128)(2,1)} %get-tuple-element.86), channel_id=1, source_target_pairs={{1,0},{2,1},{3,2},{5,4},{6,5},{7,6},{9,8},{10,9},{11,10},{13,12},{... | collective-permute-start | bytes 3145736 | tf_op jit(solution)/shard_map/ppermute | solution.py:66
  1246.7 38.9 %collective-permute-start.113 = (bf16[256,2048]{1,0:T(8,128)(2,1)}, bf16[256,2048]{1,0:T(8,128)(2,1)}, u32[]{:S(2)}, u32[]{:S(2)}) collective-permute-start(bf16[256,2048]{1,0:T(8,128)(2,1)} %get-tuple-element.85), channel_id=1, source_target_pairs={{0,1},{1,2},{2,3},{4,5},{5,6},{6,7},{8,9},{9,10},{10,11},{12,13},{... | collective-permute-start | bytes 3145736 | tf_op jit(solution)/shard_map/ppermute | solution.py:65
  1267.9 85.2 %collective-permute-start.119 = (bf16[128,4096]{1,0:T(8,128)(2,1)}, bf16[128,4096]{1,0:T(8,128)(2,1)}, u32[]{:S(2)}, u32[]{:S(2)}) collective-permute-start(bf16[128,4096]{1,0:T(8,128)(2,1)} %get-tuple-element.65), channel_id=1, source_target_pairs={{0,1},{1,2},{2,3},{4,5},{5,6},{6,7},{8,9},{9,10},{10,11},{12,13},{... | collective-permute-start | bytes 3145736 | tf_op jit(solution)/shard_map/ppermute | solution.py:65
  1306.6 46.6 %collective-permute-start.122 = (bf16[128,4096]{1,0:T(8,128)(2,1)}, bf16[128,4096]{1,0:T(8,128)(2,1)}, u32[]{:S(2)}, u32[]{:S(2)}) collective-permute-start(bf16[128,4096]{1,0:T(8,128)(2,1)} %add_convert_fusion), channel_id=1, source_target_pairs={{1,0},{2,1},{3,2},{5,4},{6,5},{7,6},{9,8},{10,9},{11,10},{13,12},{... | collective-permute-start | bytes 3145736 | tf_op jit(solution)/shard_map/ppermute | solution.py:66
  1309.7 42.8 %collective-permute-start.127 = (f32[3,2,2048]{2,0,1:T(4,128)S(1)}, f32[3,2,2048]{2,0,1:T(4,128)S(1)}, u32[]{:S(2)}, u32[]{:S(2)}) collective-permute-start(f32[3,2,2048]{2,0,1:T(4,128)S(1)} %add.588), channel_id=1, source_target_pairs={{0,2},{1,3},{2,0},{3,1},{4,6},{5,7},{6,4},{7,5},{8,10},{9,11},{10,... | collective-permute-start | bytes 147464 | tf_op jit(solution)/shard_map/ppermute | solution.py:128
  (247 other events, 5336.7 us)
Sparse Core Ops, SparseCore 0:
  11.7 84.6 all-gather.7
  98.9 33.0 all-gather.13
  133.6 134.1 all-gather.11
  269.5 86.6 all-gather.9
  357.6 110.1 all-gather.17
  469.5 56.6 all-gather.15
  640.1 69.4 reduce-scatter.10
  713.1 71.4 reduce-scatter.12
  815.7 38.7 reduce-scatter.14
  864.8 38.8 reduce-scatter.16
  906.0 115.7 reduce-scatter.8
  1101.3 39.2 reduce-scatter.22
  1144.1 71.2 reduce-scatter.18
  1218.6 61.7 reduce-scatter.20
